TPU v7x, 256 devices: a whole 4x4x8 slice. The times are simulated.
256 devices in a mesh: site: 2 (over y_lo), rows: 16 (over z, core), width: 8 (over y_hi, x).
Axes of the slice: x: 4, y: 4 (y_hi: 2, y_lo: 2; y = y_hi * 2 + y_lo), z: 8, core: 2. Of those that a mesh axis runs over, the one named last changes fastest.
Arguments:
- one_query: float32 [14336, 7168], P(('site', 'rows'), 'width'), parts along dimension 0, may hold values from -0.09375 to 0.09375
- other_query: float32 [14336, 7168], P(('site', 'rows'), 'width'), parts along dimension 0, may hold values from -0.0625 to 0.0625
- one_key: float32 [14336, 1024], P(('site', 'rows'), 'width'), parts along dimension 0, may hold values from -0.09375 to 0.09375
- other_key: float32 [14336, 1024], P(('site', 'rows'), 'width'), parts along dimension 0, may hold values from -0.0625 to 0.0625
- one_value: float32 [14336, 1024], P(('site', 'rows'), 'width'), parts along dimension 0, may hold values from -0.09375 to 0.09375
- other_value: float32 [14336, 1024], P(('site', 'rows'), 'width'), parts along dimension 0, may hold values from -0.0625 to 0.0625
- mix_share: float32 [14336], P(('site', 'rows')), parts along dimension 0, may hold values from 0.2 to 0.8
- norm_train: float32 [14336], P(('site', 'rows', 'width')), parts along dimension 0, may hold values from 0.25 to 1.75
- norm_step: float32 [14336], P(('site', 'rows', 'width')), parts along dimension 0, may hold values from -0.3 to 0.3
Outputs:
- serving_query: bfloat16 [14336, 7168], P('site', 'width'), parts along dimension 0
- serving_key: bfloat16 [14336, 1024], P('site', 'width'), parts along dimension 0
- serving_value: bfloat16 [14336, 1024], P('site', 'width'), parts along dimension 0
- scale_query: float32 [14336], P(('site', 'width')), parts along dimension 0
- scale_key: float32 [2048], P(('site', 'width')), parts along dimension 0
- scale_value: float32 [2048], P(('site', 'width')), parts along dimension 0
- serve_norm: bfloat16 [14336], P('site'), parts along dimension 0
There are 2 independent parts, one for each index of `site`. A program takes and returns all parts, laid end to end along the dimension named above; each array names one. Nothing has to cross between parts.
All inputs are finite; a program needn't handle non-finite values. Where the computation divides by a largest or mean magnitude, that divisor is 1e-20 or more.
Results may differ from a plain program's by a relative error of at most 0.001.
Values may be sent and summed in bfloat16 or wider, within the bound.
A program may use at most 128 MiB of HBM per device.

v0:
```python
import jax
import jax.numpy as jnp
from jax import lax
from jax.sharding import Mesh
from jax.sharding import PartitionSpec as P

ROWS = ("rows_0", "rows_1")
ROWS_WIDTH = ("rows_0", "rows_1", "width_0", "width_1")
SITE_ROWS = ("site", "rows_0", "rows_1")
WIDTH = ("width_0", "width_1")
SITE_ROWS_WIDTH = ("site", "rows_0", "rows_1", "width_0", "width_1")
SITE_WIDTH = ("site", "width_0", "width_1")


def copy_for_each(array, axis):
    copies = jnp.broadcast_to(array, (lax.axis_size(axis), *array.shape))
    return lax.all_to_all(copies, axis, split_axis=0, concat_axis=0, tiled=True)


def of_everyone(array, axis):
    return copy_for_each(array, axis).max(axis=0)


def packed_total(arrays, axis):
    ends = [0]
    for a in arrays:
        ends.append(ends[-1] + a.size)
    so_far = of_everyone(jnp.concatenate([a.ravel() for a in arrays]), axis)
    return tuple((so_far[b:e].reshape(a.shape) for a, b, e in zip(arrays, ends, ends[1:])))


def in_one_piece(arrays, axis, dim, along):
    both = jnp.concatenate(arrays, axis=along)
    whole, at, finished = (lax.all_gather(both, axis, axis=dim, tiled=True), 0, [])
    for a in arrays:
        finished.append(lax.slice_in_dim(whole, at, at + a.shape[along], axis=along))
        at += a.shape[along]
    return tuple(finished)


def joined_along(blocks, dim):
    lengths = list(blocks.shape[1:])
    lengths[dim] *= blocks.shape[0]
    return jnp.moveaxis(blocks, 0, dim).reshape(lengths)


def stacked_from(array, axes, turns):
    blocks = array
    for k in turns:
        blocks = lax.all_gather(blocks, axes[k])
    done = turns[::-1]
    back = [done.index(k) for k in range(len(axes))]
    blocks = blocks.transpose(*back, *range(len(axes), blocks.ndim))
    return blocks.reshape(-1, *array.shape)


def whole_of(array, axes, turns, dim):
    return joined_along(stacked_from(array, axes, turns), dim)


def shards(
    one_query,
    other_query,
    one_key,
    other_key,
    one_value,
    other_value,
    mix_share,
    norm_train,
    norm_step,
):
    whole_query = mix_share[:, None] * one_query + (1.0 - mix_share[:, None]) * other_query
    whole_key = mix_share[:, None] * one_key + (1.0 - mix_share[:, None]) * other_key
    whole_value = mix_share[:, None] * one_value + (1.0 - mix_share[:, None]) * other_value
    scale_query, scale_key, scale_value = packed_total(
        (
            jnp.max(jnp.abs(whole_query), axis=0),
            jnp.max(jnp.abs(whole_key), axis=0),
            jnp.max(jnp.abs(whole_value), axis=0),
        ),
        ROWS,
    )
    narrow_query, narrow_key, narrow_value = (
        (whole_query / scale_query).astype(jnp.bfloat16),
        (whole_key / scale_key).astype(jnp.bfloat16),
        (whole_value / scale_value).astype(jnp.bfloat16),
    )
    serving_query, serving_key, serving_value = in_one_piece(
        (narrow_query, narrow_key, narrow_value), ROWS, 0, 1
    )
    serve_norm = whole_of(
        (norm_train + norm_step).astype(jnp.bfloat16), ROWS_WIDTH, (2, 0, 3, 1), 0
    )
    return (
        serving_query,
        serving_key,
        serving_value,
        scale_query,
        scale_key,
        scale_value,
        serve_norm,
    )


def solution(mesh):
    split = Mesh(
        mesh.devices.reshape(mesh.shape["site"], 8, 2, 2, 4),
        ("site", "rows_0", "rows_1", "width_0", "width_1"),
    )
    return jax.shard_map(
        shards,
        mesh=split,
        in_specs=(
            P(SITE_ROWS, WIDTH),
            P(SITE_ROWS, WIDTH),
            P(SITE_ROWS, WIDTH),
            P(SITE_ROWS, WIDTH),
            P(SITE_ROWS, WIDTH),
            P(SITE_ROWS, WIDTH),
            P(SITE_ROWS),
            P(SITE_ROWS_WIDTH),
            P(SITE_ROWS_WIDTH),
        ),
        out_specs=(
            P("site", WIDTH),
            P("site", WIDTH),
            P("site", WIDTH),
            P(SITE_WIDTH),
            P(SITE_WIDTH),
            P(SITE_WIDTH),
            P("site"),
        ),
        check_vma=False,
    )
```

profile of v0, /device:TPU:1, one launch (start us, length us, event | category | flops | bytes accessed | tf_op | source)
XLA Modules:
  0.0 145.0 jit_solution(4714112330016848287)
XLA Ops:
  7.2 0.0 all-gather.7.cloned.1.call-start
  7.2 0.7 broadcast_subtract_fusion
  7.9 0.0 copy-start.6
  7.9 0.0 copy-start
  7.9 0.0 copy-start.1
  7.9 2.3 %abs_reduce_fusion = f32[896]{0:T(1024)S(1)} fusion(f32[448,896]{1,0:T(8,128)} %param.10, f32[448]{0:T(512)S(1)} %broadcast_subtract_fusion, f32[448,896]{1,0:T(8,128)} %param.9, f32[448]{0:T(512)} %param.15), kind=kLoop, calls=%fused_computation.1 | loop fusion | flops 2006144 | bytes 3218432 | tf_op jit(solution)/shard_map/reduce_max | solution.py:77
  10.2 0.0 copy-done.6
  10.2 1.5 %abs_reduce_fusion.2 = (f32[128]{0:T(128)S(1)}, f32[128]{0:T(128)S(1)}) fusion(f32[448,128]{1,0:T(8,128)} %param.12, f32[448]{0:T(512)S(1)} %broadcast_subtract_fusion, f32[448,128]{1,0:T(8,128)} %param.11, f32[448]{0:T(512)S(1)} %copy-done.6, f32[448,128]{1,0:T(8,128)} %param.14, f32[448,128]{1,0:T(8,128)} %param.13), kind=kLoop, calls=%fused_computation.8 | loop fusion | flops 573184 | bytes 922112 | tf_op jit(solution)/shard_map/reduce_max | solution.py:78
  11.8 17.7 %all_to_all.6 = f32[16,1,1152]{2,1,0:T(1,128)S(1)} all-to-all(f32[16,1,1152]{2,1,0:T(1,128)S(1)} %broadcast_in_dim.2), channel_id=1, replica_groups=mesh['site'=2,'rows_0'=8,'rows_1'=2,'width_0'=2,'width_1'=4] {'rows_0','..., dimensions={0} | all-to-all | bytes 147456 | tf_op jit(solution)/shard_map/all_to_all | solution.py:17
  29.5 0.1 reduce_max.39
  29.6 0.0 copy-start.8
  29.6 0.0 copy-start.9
  29.6 0.0 copy-done
  29.6 0.0 copy-done.1
  29.6 0.0 copy-start.7
  29.6 0.0 copy-start.2
  29.6 0.0 copy-start.3
  29.7 0.0 copy-start.4
  29.7 0.0 copy-start.5
  29.7 0.3 divide_convert_fusion
  30.0 0.2 copy-done.7
  30.2 0.0 copy-done.8
  30.2 0.0 copy-done.9
  30.2 0.4 copy-done.2
  30.6 0.1 copy-done.3
  30.7 0.1 copy-done.4
  30.8 0.1 copy-done.5
  30.9 0.2 divide_convert_fusion.2
  31.1 0.0 copy-start.12
  31.1 0.0 copy-start.10
  31.1 0.0 copy-start.11
  31.2 1.1 pad_maximum_fusion
  32.2 0.0 all-gather.7.cloned.1.call-update
  32.2 0.0 copy-done.12
  32.2 0.6 dynamic-slice
  33.5 0.0 copy-done.10
  33.5 0.0 copy-done.11
  33.5 0.2 dynamic-update-slice
  33.8 5.3 %all-reduce = bf16[112]{0:T(256)(128)(2,1)S(1)} all-reduce(bf16[112]{0:T(256)(128)(2,1)S(1)} %dynamic-update-slice), channel_id=2, replica_groups=mesh['site'=2,'rows_0'=8,'rows_1'=2,'width_0'=2,'width_1'=4] {'width_0'}, use_global_device_ids=true, to_apply=%add | all-reduce | flops 112 | bytes 448
  39.0 0.1 reshape.31
  39.1 11.5 %all-gather.4 = bf16[8,2,56]{2,1,0:T(2,128)(2,1)S(1)} all-gather(bf16[1,2,56]{2,1,0:T(2,128)(2,1)S(1)} %reshape.31), channel_id=3, replica_groups=mesh['site'=2,'rows_0'=8,'rows_1'=2,'width_0'=2,'width_1'=4] {'rows_0'}, dimensions={0}, use_global_device_ids=true | all-gather | bytes 2016 | tf_op jit(solution)/shard_map/all_gather | solution.py:50
  50.6 10.4 %all-gather.2 = bf16[32,2,56]{2,1,0:T(2,128)(2,1)S(1)} all-gather(bf16[8,2,56]{2,1,0:T(2,128)(2,1)S(1)} %all-gather.4), channel_id=4, replica_groups=mesh['site'=2,'rows_0'=8,'rows_1'=2,'width_0'=2,'width_1'=4] {'width_1'}, dimensions={0}, use_global_device_ids=true | all-gather | bytes 8960 | tf_op jit(solution)/shard_map/all_gather | solution.py:50
  61.0 7.5 %all-gather.3 = bf16[8,8,2,56]{3,1,2,0:T(8,128)(2,1)S(1)} all-gather(bf16[4,8,2,56]{3,1,2,0:T(8,128)(2,1)S(1)} %copy.23), channel_id=5, replica_groups=mesh['site'=2,'rows_0'=8,'rows_1'=2,'width_0'=2,'width_1'=4] {'rows_1'}, dimensions={0}, use_global_device_ids=true | all-gather | bytes 21504 | tf_op jit(solution)/shard_map/all_gather | solution.py:50
  68.5 0.7 reshape_reshape.3
  69.2 54.1 %all-gather.7.cloned.1.call-done = bf16[7168,1152]{1,0:T(8,128)(2,1)} async-done(((bf16[448,1152]{1,0:T(8,128)(2,1)}), bf16[7168,1152]{1,0:T(8,128)(2,1)}) %all-gather.7.cloned.1.call-update) | async-done | bytes 16515088 | tf_op jit(solution)/shard_map/all_gather | solution.py:34
  123.4 10.7 %slice.27 = bf16[7168,896]{1,0:T(8,128)(2,1)} slice(bf16[7168,1152]{1,0:T(8,128)(2,1)} %all-gather.7.cloned.1.call-done), slice={[0:7168], [0:896]} | slice | bytes 25690112 | tf_op jit(solution)/shard_map/slice | solution.py:36
  134.0 4.1 %fusion = (bf16[7168,128]{1,0:T(8,128)(2,1)}, bf16[7168,128]{1,0:T(8,128)(2,1)}) fusion(bf16[7168,1152]{1,0:T(8,128)(2,1)} %all-gather.7.cloned.1.call-done), kind=kLoop, calls=%fused_computation.13 | loop fusion | bytes 7340032 | tf_op jit(solution)/shard_map/slice | solution.py:36
  (8 shorter events, 0.1 us)
Async XLA Ops:
  7.2 116.2 %all-gather.7.cloned.1.call-start = ((), (), s32[]{:S(2)}) async-start(), calls=%async_computation.1 | async-start | bytes 17547264 | tf_op jit(solution)/shard_map/all_gather | solution.py:34
  7.9 2.3 %copy-start.6 = (f32[448]{0:T(512)S(1)}, f32[448]{0:T(512)}, u32[]{:S(2)}) copy-start(f32[448]{0:T(512)} %param.15) | copy-start | bytes 5380
  7.9 21.7 %copy-start = (f32[448,896]{1,0:T(8,128)S(1)}, f32[448,896]{1,0:T(8,128)}, u32[]{:S(2)}) copy-start(f32[448,896]{1,0:T(8,128)} %param.10) | copy-start | bytes 4816900
  7.9 21.7 %copy-start.1 = (f32[448,896]{1,0:T(8,128)S(1)}, f32[448,896]{1,0:T(8,128)}, u32[]{:S(2)}) copy-start(f32[448,896]{1,0:T(8,128)} %param.9) | copy-start | bytes 4816900
  29.6 0.7 copy-start.8
  29.6 0.6 copy-start.9
  29.6 0.6 copy-start.7
  29.6 0.9 copy-start.2
  29.6 1.0 copy-start.3
  29.7 1.1 copy-start.4
  29.7 1.3 copy-start.5
  31.1 1.1 copy-start.12
  31.1 2.4 %copy-start.10 = (f32[56]{0:T(128)S(1)}, f32[56]{0:T(128)}, u32[]{:S(2)}) copy-start(f32[56]{0:T(128)} %param.16) | copy-start | bytes 676
  31.1 2.4 %copy-start.11 = (f32[56]{0:T(128)S(1)}, f32[56]{0:T(128)}, u32[]{:S(2)}) copy-start(f32[56]{0:T(128)} %param.17) | copy-start | bytes 676
Sparse Core Ops, SparseCore 0:
  32.4 90.9 all-gather.6
where the time goes:
time: 145 us
  waiting for transfers between devices  54.1 us (37%)
  blocking collectives  52.3 us (36%)
  local copies, waits for them, and re-layouts  17.5 us (12%)
  between operations  14.9 us (10%)
  other arithmetic  6.11 us (4%)
    all_gather x1, waiting for transfers between devices, in_one_piece(): lax.all_gather(both, axis, axis=dim, tiled=True)  54.1 us
    all_gather x3, blocking collectives, stacked_from(): blocks = lax.all_gather(blocks, axes[k])  29.4 us
    all_to_all x1, blocking collectives, copy_for_each(): return lax.all_to_all(copies, axis, split_axis=0, concat_axis=0, tiled=True)  17.7 us
    slice x2, local copies, waits for them, and re-layouts, in_one_piece(): lax.slice_in_dim(whole, at, at + a.shape[along], axis=along)  14.8 us
    unnamed x1, blocking collectives  5.26 us
  transfers between devices with their start and end apart: 1, of which 1 were waited for; matrix products, arithmetic and copies ran while one was open for 1% of the time, Pallas kernels for 0%

commit v1 on v0

v1 whole, which is shorter than its diff:
```python
import functools

import jax
import jax.numpy as jnp
from jax import lax
from jax.experimental import pallas as pl
from jax.experimental.pallas import tpu as pltpu
from jax.sharding import PartitionSpec as P

MESH = pl.DeviceIdType.MESH
LANES = 128
LOAD = 64


def bounds_of(rows):
    half = rows // 2
    cuts = [0, half // 2, half, half + half // 2, rows]
    return list(zip(cuts, cuts[1:]))


def gather_kernel(nrows, nwidth, dims, *refs):
    (one_q, other_q, one_k, other_k, one_v, other_v, mix_hbm, norm_t_hbm, norm_s_hbm,
     out, scale_q, scale_k, scale_v, norm_out,
     mix, norm_t, norm_s, a_buf, b_buf, mixb, acc, maxima, seg, tiles_w, tiles_r, joined,
     lead_sem, in_sem, max_send, max_recv, nw_send, nw_recv, nr_send, nr_recv,
     ring_send, ring_recv, share_send, share_recv) = refs
    rows, qd, kd = dims
    cols = qd + 2 * kd
    nz = nrows // 2
    r = lax.axis_index("rows")
    w = lax.axis_index("width")
    z, c = r // 2, lax.rem(r, 2)
    bounds = bounds_of(rows)
    nchunk = len(bounds)

    def row_peer(i):
        return {"rows": lax.rem(r + i, nrows)}

    def width_peer(i):
        return {"width": lax.rem(w + i, nwidth)}

    barrier = pltpu.get_barrier_semaphore()
    for i in range(1, nrows):
        pl.semaphore_signal(barrier, inc=1, device_id=row_peer(i), device_id_type=MESH)
    for i in range(1, nwidth):
        pl.semaphore_signal(barrier, inc=1, device_id=width_peer(i), device_id_type=MESH)

    leads = [
        pltpu.make_async_copy(src, dst, lead_sem.at[i])
        for i, (src, dst) in enumerate(((mix_hbm, mix), (norm_t_hbm, norm_t), (norm_s_hbm, norm_s)))
    ]
    for copy in leads:
        copy.start()
    parts = (
        (one_q, a_buf, 0, qd), (other_q, b_buf, 0, qd),
        (one_k, a_buf, qd, kd), (other_k, b_buf, qd, kd),
        (one_v, a_buf, qd + kd, kd), (other_v, b_buf, qd + kd, kd),
    )

    def loads(step):
        span = pl.ds(step * LOAD, LOAD)
        return [
            pltpu.make_async_copy(src.at[span, :], dst.at[span, pl.ds(at, n)], in_sem.at[step, i])
            for i, (src, dst, at, n) in enumerate(parts)
        ]

    for step in range(rows // LOAD):
        for copy in loads(step):
            copy.start()

    for copy in leads:
        copy.wait()

    for at in range(0, rows, LANES):
        n = min(LANES, rows - at)
        line = mix[:, at:at + n]
        if n < LANES:
            line = jnp.concatenate([line, jnp.zeros((1, LANES - n), jnp.float32)], axis=1)
        square = jnp.transpose(jnp.broadcast_to(line, (LANES, LANES)))
        mixb[at:at + n, :] = square[:n, :]

    small = norm_t.shape[1]
    pos = lax.rem(r, 2) * nwidth + w
    first, lane0 = (pos * small) // LANES, lax.rem(pos * small, LANES)
    seg[...] = jnp.zeros((8, LANES), jnp.float32)
    seg[0:1, 0:small] = norm_t[...] + norm_s[...]
    turned = pltpu.roll(seg[...], lane0, 1)[0:1, :]
    lane = lax.broadcasted_iota(jnp.int32, (8, LANES), 1)
    line = lax.broadcasted_iota(jnp.int32, (8, LANES), 0)
    here = ((line == first) & (lane >= lane0)) | ((line == first + 1) & (lane < lane0))
    tiles_w[w] = jnp.where(here, jnp.broadcast_to(turned, (8, LANES)), 0.0)

    acc[...] = jnp.zeros((8, cols), jnp.float32)
    for step in range(rows // LOAD):
        for copy in loads(step):
            copy.wait()
        span = slice(step * LOAD, (step + 1) * LOAD)
        m = mixb[span, :]
        rest = 1.0 - m
        for at in range(0, cols, LANES):
            lanes = slice(at, at + LANES)
            whole = m * a_buf[span, lanes] + rest * b_buf[span, lanes]
            a_buf[span, lanes] = whole
            top = jnp.max(jnp.abs(whole).reshape(LOAD // 8, 8, LANES), axis=0)
            acc[:, lanes] = jnp.maximum(acc[:, lanes], top)
    maxima[r] = jnp.max(acc[...], axis=0, keepdims=True)

    pl.semaphore_wait(barrier, nrows - 1 + nwidth - 1)

    order = sorted(range(1, nrows), key=lambda i: -min(i, nrows - i))

    def max_copy(i):
        return pltpu.make_async_remote_copy(
            src_ref=maxima.at[r], dst_ref=maxima.at[r], send_sem=max_send.at[i], recv_sem=max_recv.at[i],
            device_id=row_peer(i), device_id_type=MESH)

    def norm_w_copy(i):
        return pltpu.make_async_remote_copy(
            src_ref=tiles_w.at[w], dst_ref=tiles_w.at[w], send_sem=nw_send.at[i], recv_sem=nw_recv.at[i],
            device_id=width_peer(i), device_id_type=MESH)

    def norm_r_copy(i):
        return pltpu.make_async_remote_copy(
            src_ref=tiles_r.at[r], dst_ref=tiles_r.at[r], send_sem=nr_send.at[i], recv_sem=nr_recv.at[i],
            device_id=row_peer(i), device_id_type=MESH)

    for i in order:
        max_copy(i).start()
    for i in range(1, nwidth):
        norm_w_copy(i).start()
    for i in order:
        max_copy(i).wait_recv()
    scale = maxima[0]
    for i in range(1, nrows):
        scale = jnp.maximum(scale, maxima[i])
    for line in range(qd // LANES):
        scale_q[line:line + 1, :] = scale[:, line * LANES:(line + 1) * LANES]
    scale_k[...] = scale[:, qd:qd + kd]
    scale_v[...] = scale[:, qd + kd:]

    steps = (1, nrows - 1), (nz // 2, nz // 2)
    ahead = ({"rows": lax.rem(r + 2, nrows)}, {"rows": lax.rem(r + nrows - 2, nrows)})
    partner = {"rows": r + 1 - 2 * c}

    def block(direction, hop, chunk):
        lo, hi = bounds[chunk]
        owner = lax.rem(z - hop + nz, nz) if direction == 0 else lax.rem(z + hop, nz)
        at = (owner * 2 + c) * rows + lo
        return out.at[pl.ds(pl.multiple_of(at, 16), hi - lo), :]

    def ring(direction, hop, chunk):
        ref = block(direction, hop, chunk)
        return pltpu.make_async_remote_copy(
            src_ref=ref, dst_ref=ref, send_sem=ring_send.at[direction, hop, chunk],
            recv_sem=ring_recv.at[direction, hop, chunk], device_id=ahead[direction], device_id_type=MESH)

    def arrived(direction, hop, chunk):
        ref = block(direction, hop, chunk)
        return pltpu.make_async_remote_copy(
            src_ref=ref, dst_ref=ref, send_sem=ring_send.at[direction, hop - 1, chunk],
            recv_sem=ring_recv.at[direction, hop - 1, chunk], device_id=ahead[direction], device_id_type=MESH)

    def share(direction, hop, chunk):
        ref = block(direction, hop, chunk)
        return pltpu.make_async_remote_copy(
            src_ref=ref, dst_ref=ref, send_sem=share_send.at[direction, hop, chunk],
            recv_sem=share_recv.at[direction, hop, chunk], device_id=partner, device_id_type=MESH)

    far = nz // 2

    def chunks(direction, hop):
        if hop < far:
            return list(range(nchunk))
        return list(range(nchunk // 2)) if direction == 0 else list(range(nchunk // 2, nchunk))

    mine = r * rows
    for chunk, (lo, hi) in enumerate(bounds):
        for at in range(0, cols, LANES):
            lanes = slice(at, at + LANES)
            out[pl.ds(pl.multiple_of(mine + lo, 16), hi - lo), lanes] = (
                a_buf[lo:hi, lanes] / scale[:, lanes]).astype(out.dtype)
        ring(0, 0, chunk).start()
        ring(1, 0, chunk).start()
        share(0, 0, chunk).start()

    for i in range(1, nwidth):
        norm_w_copy(i).wait_recv()
    total = tiles_w[0]
    for i in range(1, nwidth):
        total = total + tiles_w[i]
    tiles_r[r] = total
    for i in order:
        norm_r_copy(i).start()

    for hop in range(1, far + 1):
        for pair in zip(*(chunks(d, hop) for d in (0, 1))):
            for direction, chunk in enumerate(pair):
                arrived(direction, hop, chunk).wait_recv()
                if hop + 1 <= far and chunk in chunks(direction, hop + 1):
                    ring(direction, hop, chunk).start()
                share(direction, hop, chunk).start()
        if hop == 1:
            for i in order:
                norm_r_copy(i).wait_recv()
            per = 2 * nwidth * small // LANES
            for g in range(nrows // 2):
                full = tiles_r[2 * g] + tiles_r[2 * g + 1]
                joined[g * per:(g + 1) * per, :] = full[:per, :]
            norm_out[...] = joined[...].astype(norm_out.dtype)

    for hop in range(far + 1):
        for direction in (0, 1) if hop else (0,):
            for chunk in chunks(direction, hop):
                lo, hi = bounds[chunk]
                owner = lax.rem(z - hop + nz, nz) if direction == 0 else lax.rem(z + hop, nz)
                at = (owner * 2 + 1 - c) * rows + lo
                ref = out.at[pl.ds(pl.multiple_of(at, 16), hi - lo), :]
                pltpu.make_async_remote_copy(
                    src_ref=ref, dst_ref=ref, send_sem=share_send.at[direction, hop, chunk],
                    recv_sem=share_recv.at[direction, hop, chunk], device_id=partner,
                    device_id_type=MESH).wait_recv()
                share(direction, hop, chunk).wait_send()
    for hop in range(far):
        for direction in (0, 1):
            for chunk in chunks(direction, hop + 1):
                ring(direction, hop, chunk).wait_send()
    for i in range(1, nrows):
        max_copy(i).wait_send()
        norm_r_copy(i).wait_send()
    for i in range(1, nwidth):
        norm_w_copy(i).wait_send()


def write_kernel(dims, full, *refs):
    qd, kd = dims
    q, k, v = refs[4:7]
    sems = refs[-1]
    rows = full.shape[0]
    pieces = 8
    step = rows // pieces
    copies = []
    for i in range(pieces):
        span = pl.ds(i * step, step)
        copies.append((full.at[span, pl.ds(0, qd)], q.at[span, :]))
        copies.append((full.at[span, pl.ds(qd, kd)], k.at[span, :]))
        copies.append((full.at[span, pl.ds(qd + kd, kd)], v.at[span, :]))
    copies.extend(zip(refs[:4], refs[7:11]))
    started = [pltpu.make_async_copy(src, dst, sems.at[i]) for i, (src, dst) in enumerate(copies)]
    for copy in started:
        copy.start()
    for copy in started:
        copy.wait()


def shards(nrows, nwidth, one_q, other_q, one_k, other_k, one_v, other_v, mix, norm_t, norm_s):
    rows, qd = one_q.shape
    kd = one_k.shape[1]
    cols = qd + 2 * kd
    small = norm_t.shape[0]
    total = rows * nrows
    lines = small * nrows * nwidth // LANES
    nz, nchunk = nrows // 2, len(bounds_of(rows))
    far = nz // 2
    hbm = pl.BlockSpec(memory_space=pltpu.HBM)
    vmem = pl.BlockSpec(memory_space=pltpu.VMEM)
    full, scale_q, scale_k, scale_v, norm = pl.pallas_call(
        functools.partial(gather_kernel, nrows, nwidth, (rows, qd, kd)),
        out_shape=(
            pltpu.VMEM((total, cols), jnp.bfloat16),
            pltpu.VMEM((qd // LANES, LANES), jnp.float32),
            pltpu.VMEM((1, kd), jnp.float32),
            pltpu.VMEM((1, kd), jnp.float32),
            pltpu.VMEM((lines, LANES), jnp.bfloat16),
        ),
        in_specs=[hbm] * 9,
        out_specs=(vmem,) * 5,
        scratch_shapes=[
            pltpu.VMEM((1, rows), jnp.float32),
            pltpu.VMEM((1, small), jnp.float32),
            pltpu.VMEM((1, small), jnp.float32),
            pltpu.VMEM((rows, cols), jnp.float32),
            pltpu.VMEM((rows, cols), jnp.float32),
            pltpu.VMEM((rows, LANES), jnp.float32),
            pltpu.VMEM((8, cols), jnp.float32),
            pltpu.VMEM((nrows, 1, cols), jnp.float32),
            pltpu.VMEM((8, LANES), jnp.float32),
            pltpu.VMEM((nwidth, 8, LANES), jnp.float32),
            pltpu.VMEM((nrows, 8, LANES), jnp.float32),
            pltpu.VMEM((lines, LANES), jnp.float32),
            pltpu.SemaphoreType.DMA((3,)),
            pltpu.SemaphoreType.DMA((rows // LOAD, 6)),
            pltpu.SemaphoreType.DMA((nrows,)),
            pltpu.SemaphoreType.DMA((nrows,)),
            pltpu.SemaphoreType.DMA((nwidth,)),
            pltpu.SemaphoreType.DMA((nwidth,)),
            pltpu.SemaphoreType.DMA((nrows,)),
            pltpu.SemaphoreType.DMA((nrows,)),
            pltpu.SemaphoreType.DMA((2, far, nchunk)),
            pltpu.SemaphoreType.DMA((2, far, nchunk)),
            pltpu.SemaphoreType.DMA((2, far + 1, nchunk)),
            pltpu.SemaphoreType.DMA((2, far + 1, nchunk)),
        ],
        compiler_params=pltpu.CompilerParams(
            collective_id=0, has_side_effects=True, vmem_limit_bytes=24 * 1024 * 1024),
        name="gather",
    )(*(pltpu.with_memory_space_constraint(x, pltpu.HBM) for x in (
        one_q, other_q, one_k, other_k, one_v, other_v,
        mix.reshape(1, -1), norm_t.reshape(1, -1), norm_s.reshape(1, -1))))
    q, k, v, scale_q, scale_k, scale_v, norm_o = pl.pallas_call(
        functools.partial(write_kernel, (qd, kd)),
        out_shape=(
            jax.ShapeDtypeStruct((total, qd), jnp.bfloat16),
            jax.ShapeDtypeStruct((total, kd), jnp.bfloat16),
            jax.ShapeDtypeStruct((total, kd), jnp.bfloat16),
            jax.ShapeDtypeStruct((qd // LANES, LANES), jnp.float32),
            jax.ShapeDtypeStruct((1, kd), jnp.float32),
            jax.ShapeDtypeStruct((1, kd), jnp.float32),
            jax.ShapeDtypeStruct((lines, LANES), jnp.bfloat16),
        ),
        in_specs=[vmem] * 5,
        out_specs=(hbm,) * 7,
        scratch_shapes=[pltpu.SemaphoreType.DMA((28,))],
        compiler_params=pltpu.CompilerParams(vmem_limit_bytes=1024 * 1024),
        name="write",
    )(full, scale_q, scale_k, scale_v, norm)
    return (q, k, v, scale_q.reshape(-1), scale_k.reshape(-1), scale_v.reshape(-1),
            norm_o.reshape(-1))


def solution(mesh):
    rows = ("site", "rows")
    return jax.shard_map(
        functools.partial(shards, mesh.shape["rows"], mesh.shape["width"]),
        mesh=mesh,
        in_specs=(P(rows, "width"),) * 6 + (P(rows), P(("site", "rows", "width")), P(("site", "rows", "width"))),
        out_specs=(P("site", "width"),) * 3 + (P(("site", "width")),) * 3 + (P("site"),),
        check_vma=False,
    )
```

time: 145 us -> 108 us (0.74)
  Pallas kernels: 0 us -> 107 us
  waiting for transfers between devices: 54.1 us -> 0 us
  blocking collectives: 52.3 us -> 0 us
  local copies, waits for them, and re-layouts: 17.5 us -> 0 us
  between operations: 14.9 us -> 0.64 us
  other arithmetic: 6.11 us -> 0 us
    pallas_call x0 -> x2, Pallas kernels: none -> 107 us  [the longest x1 101 us: shards(): pl.pallas_call(functools.partial(gather_kernel, nrows, nwidth, (rows, qd,...]
    all_gather x1 -> x0, waiting for transfers between devices: 54.1 us -> none  [in_one_piece(): lax.all_gather(both, axis, axis=dim, tiled=True)]
    all_gather x3 -> x0, blocking collectives: 29.4 us -> none  [stacked_from(): blocks = lax.all_gather(blocks, axes[k])]
    all_to_all x1 -> x0, blocking collectives: 17.7 us -> none  [copy_for_each(): return lax.all_to_all(copies, axis, split_axis=0, concat_axis=0, tiled=True)]
    slice x4 -> x0, local copies, waits for them, and re-layouts: 14.8 us -> none  [the longest x2 14.8 us: in_one_piece(): lax.slice_in_dim(whole, at, at + a.shape[along], axis=along)]
    unnamed x1 -> x0, blocking collectives: 5.26 us -> none
    reduce_max x3 -> x0, other arithmetic: 3.86 us -> none  [the longest x1 2.32 us: shards(): jnp.max(jnp.abs(whole_query), axis=0)]
    unnamed x30 -> x0, local copies, waits for them, and re-layouts: 1.9 us -> none
  transfers between devices with their start and end apart: 1 -> 0, of which waited for: 1 -> 0; matrix products, arithmetic and copies ran while one was open for 1% -> 0% of each run, Pallas kernels for 0% -> 0%
where the time goes in v1:
time: 108 us; the launch traced here: 107 us
  Pallas kernels  107 us (99%)
    pallas_call x1, Pallas kernels, shards(): pl.pallas_call(functools.partial(gather_kernel, nrows, nwidth, (rows, qd,...  101 us
    pallas_call x1, Pallas kernels, shards(): pl.pallas_call(functools.partial(write_kernel, (qd, kd)), out_shape=(jax....  6.01 us

profile of v1, /device:TPU:1, one launch (start us, length us, event | category | flops | bytes accessed | tf_op | source)
XLA Modules:
  0.0 107.4 jit_solution(7957137064692554782)
XLA Ops:
  0.6 100.8 %gather.1 = (bf16[7168,1152]{1,0:T(8,128)(2,1)S(1)}, f32[7,128]{1,0:T(8,128)S(1)}, f32[1,128]{1,0:T(1,128)S(1)}, f32[1,128]{1,0:T(1,128)S(1)}, bf16[56,128]{1,0:T(8,128)(2,1)S(1)}) custom-call(f32[448,896]{1,0:T(8,128)} %refs_0_.1, f32[448,896]{1,0:T(8,128)} %refs_1_.1, f32[448,128]{1,0:T(8,128)} %refs_2_.1, f32[448,128]{1,0:T(8,128)} %refs_3_.1, ...), custom_call_target="tpu_custom_call" | custom-call | tf_op jit(solution)/shard_map/gather/pallas_call | solution.py:266
  101.4 6.0 %write.1 = (bf16[7168,896]{1,0:T(8,128)(2,1)}, bf16[7168,128]{1,0:T(8,128)(2,1)}, bf16[7168,128]{1,0:T(8,128)(2,1)}, f32[7,128]{1,0:T(8,128)}, f32[1,128]{1,0:T(...) custom-call(bf16[7168,1152]{1,0:T(8,128)(2,1)S(1)} %get-tuple-element.19.full, ...), custom_call_target="tpu_custom_call" | custom-call | tf_op jit(solution)/shard_map/write/pallas_call | solution.py:309

commit v2 on v1

v2 whole, which is shorter than its diff:
```python
import functools

import jax
import jax.numpy as jnp
from jax import lax
from jax.experimental import pallas as pl
from jax.experimental.pallas import tpu as pltpu
from jax.sharding import PartitionSpec as P

MESH = pl.DeviceIdType.MESH
LANES = 128
LOAD = 56
ROOT = 1


def bounds_of(rows):
    half = rows // 2
    cuts = [0, half // 2, half - 32, half]
    cuts += [half + at for at in cuts[1:]]
    return list(zip(cuts, cuts[1:]))


def gather_kernel(nrows, nwidth, dims, *refs):
    (one_q, other_q, one_k, other_k, one_v, other_v, mix_hbm, norm_t_hbm, norm_s_hbm,
     out, scale_q, scale_k, scale_v, norm_out,
     mix, norm_t, norm_s, a_buf, b_buf, early, mixb, acc, maxima, seg, tiles, gains, joined,
     tokens, lead_sem, in_sem, max_send, max_recv, tile_send, tile_recv, gain_send, gain_recv, norm_send, norm_recv,
     early_send, early_recv, ring_send, ring_recv, share_send, share_recv) = refs
    rows, qd, kd = dims
    cols = qd + 2 * kd
    nz = nrows // 2
    far = nz // 2
    r = lax.axis_index("rows")
    w = lax.axis_index("width")
    z, c = r // 2, lax.rem(r, 2)
    bounds = bounds_of(rows)
    nchunk = len(bounds)
    early_rows = bounds[0][1]
    is_root = r == ROOT

    def row_peer(i):
        return {"rows": lax.rem(r + i, nrows)}

    def width_peer(i):
        return {"width": lax.rem(w + i, nwidth)}

    ahead = (row_peer(2), row_peer(nrows - 2))
    partner = {"rows": r + 1 - 2 * c}

    barrier = pltpu.get_barrier_semaphore()
    for dz in (1, nz - 1):
        for core in (0, 1):
            pl.semaphore_signal(
                barrier, inc=1, device_id={"rows": lax.rem(z + dz, nz) * 2 + core}, device_id_type=MESH)
    pl.semaphore_signal(barrier, inc=1, device_id=partner, device_id_type=MESH)

    @pl.when(is_root)
    def _():
        for i in range(1, nwidth):
            pl.semaphore_signal(barrier, inc=1, device_id=width_peer(i), device_id_type=MESH)

    leads = [
        pltpu.make_async_copy(src, dst, lead_sem.at[i])
        for i, (src, dst) in enumerate(((mix_hbm, mix), (norm_t_hbm, norm_t), (norm_s_hbm, norm_s)))
    ]
    for copy in leads:
        copy.start()
    parts = (
        (one_q, a_buf, 0, qd), (other_q, b_buf, 0, qd),
        (one_k, a_buf, qd, kd), (other_k, b_buf, qd, kd),
        (one_v, a_buf, qd + kd, kd), (other_v, b_buf, qd + kd, kd),
    )

    def loads(step):
        span = pl.ds(step * LOAD, LOAD)
        return [
            pltpu.make_async_copy(src.at[span, :], dst.at[span, pl.ds(at, n)], in_sem.at[step, i])
            for i, (src, dst, at, n) in enumerate(parts)
        ]

    for step in range(rows // LOAD):
        for copy in loads(step):
            copy.start()
    for copy in leads:
        copy.wait()

    for at in range(0, rows, LANES):
        n = min(LANES, rows - at)
        line = mix[:, at:at + n]
        if n < LANES:
            line = jnp.concatenate([line, jnp.zeros((1, LANES - n), jnp.float32)], axis=1)
        square = jnp.transpose(jnp.broadcast_to(line, (LANES, LANES)))
        mixb[at:at + n, :] = square[:n, :]

    def early_copy(direction, piece):
        span = pl.ds(piece * LOAD, LOAD)
        return pltpu.make_async_remote_copy(
            src_ref=a_buf.at[span, :], dst_ref=early.at[direction, span, :], send_sem=early_send.at[direction, piece],
            recv_sem=early_recv.at[direction, piece], device_id=ahead[direction], device_id_type=MESH)

    acc[...] = jnp.zeros((8, cols), jnp.float32)
    for step in range(rows // LOAD):
        for copy in loads(step):
            copy.wait()
        span = slice(step * LOAD, (step + 1) * LOAD)
        m = mixb[span, :]
        rest = 1.0 - m
        for at in range(0, cols, LANES):
            lanes = slice(at, at + LANES)
            whole = m * a_buf[span, lanes] + rest * b_buf[span, lanes]
            a_buf[span, lanes] = whole
            top = jnp.max(jnp.abs(whole).reshape(LOAD // 8, 8, LANES), axis=0)
            acc[:, lanes] = jnp.maximum(acc[:, lanes], top)
        if step == 0:
            pl.semaphore_wait(barrier, 5 + jnp.where(is_root, nwidth - 1, 0))
            for direction in (0, 1):
                pl.semaphore_signal(tokens.at[direction, 2], inc=1, device_id=ahead[direction], device_id_type=MESH)
        if (step + 1) * LOAD <= early_rows:
            for direction in (0, 1):
                early_copy(direction, step).start()
    maxima[r] = jnp.max(acc[...], axis=0, keepdims=True)

    for hop in range(2, far + 1):
        for direction in (0, 1):
            pl.semaphore_wait(tokens.at[direction, hop], 1)
            if hop < far:
                pl.semaphore_signal(
                    tokens.at[direction, hop + 1], inc=1, device_id=ahead[direction], device_id_type=MESH)

    order = sorted(range(1, nrows), key=lambda i: -min(i, nrows - i))

    def max_copy(i):
        return pltpu.make_async_remote_copy(
            src_ref=maxima.at[r], dst_ref=maxima.at[r], send_sem=max_send.at[i], recv_sem=max_recv.at[i],
            device_id=row_peer(i), device_id_type=MESH)

    for i in order:
        max_copy(i).start()

    small = norm_t.shape[1]
    pos = lax.rem(r, 2) * nwidth + w
    first, lane0 = (pos * small) // LANES, lax.rem(pos * small, LANES)
    seg[...] = jnp.zeros((8, LANES), jnp.float32)
    seg[0:1, 0:small] = norm_t[...] + norm_s[...]
    turned = pltpu.roll(seg[...], lane0, 1)[0:1, :]
    lane = lax.broadcasted_iota(jnp.int32, (8, LANES), 1)
    line = lax.broadcasted_iota(jnp.int32, (8, LANES), 0)
    here = ((line == first) & (lane >= lane0)) | ((line == first + 1) & (lane < lane0))
    tiles[r] = jnp.where(here, jnp.broadcast_to(turned, (8, LANES)), 0.0)

    def tile_copy(source):
        return pltpu.make_async_remote_copy(
            src_ref=tiles.at[source], dst_ref=tiles.at[source], send_sem=tile_send, recv_sem=tile_recv.at[source],
            device_id={"rows": ROOT}, device_id_type=MESH)

    def gain_copy(i):
        return pltpu.make_async_remote_copy(
            src_ref=gains.at[w], dst_ref=gains.at[w], send_sem=gain_send.at[i], recv_sem=gain_recv.at[i],
            device_id=width_peer(i), device_id_type=MESH)

    def norm_copy(i):
        return pltpu.make_async_remote_copy(
            src_ref=norm_out, dst_ref=norm_out, send_sem=norm_send.at[i], recv_sem=norm_recv,
            device_id=row_peer(i), device_id_type=MESH)

    @pl.when(jnp.logical_not(is_root))
    def _():
        tile_copy(r).start()

    for i in order:
        max_copy(i).wait_recv()
    scale = maxima[0]
    for i in range(1, nrows):
        scale = jnp.maximum(scale, maxima[i])

    def place(direction, hop, core, chunk):
        lo, hi = bounds[chunk]
        owner = lax.rem(z - hop + nz, nz) if direction == 0 else lax.rem(z + hop, nz)
        return pl.ds(pl.multiple_of((owner * 2 + core) * rows + lo, 16), hi - lo)

    def ring(direction, hop, chunk):
        ref = out.at[place(direction, hop, c, chunk), :]
        return pltpu.make_async_remote_copy(
            src_ref=ref, dst_ref=ref, send_sem=ring_send.at[direction, hop, chunk],
            recv_sem=ring_recv.at[direction, hop, chunk], device_id=ahead[direction], device_id_type=MESH)

    def arrived(direction, hop, chunk):
        ref = out.at[place(direction, hop, c, chunk), :]
        return pltpu.make_async_remote_copy(
            src_ref=ref, dst_ref=ref, send_sem=ring_send.at[direction, hop - 1, chunk],
            recv_sem=ring_recv.at[direction, hop - 1, chunk], device_id=ahead[direction], device_id_type=MESH)

    def share(direction, hop, chunk, core):
        ref = out.at[place(direction, hop, core, chunk), :]
        return pltpu.make_async_remote_copy(
            src_ref=ref, dst_ref=ref, send_sem=share_send.at[direction, hop, chunk],
            recv_sem=share_recv.at[direction, hop, chunk], device_id=partner, device_id_type=MESH)

    def chunks(direction, hop):
        if hop < far:
            return list(range(nchunk))
        return list(range(nchunk // 2)) if direction == 0 else list(range(nchunk // 2, nchunk))

    def rounded(source, direction, hop, chunk):
        at_rows = place(direction, hop, c, chunk)
        for at in range(0, cols, LANES):
            lanes = slice(at, at + LANES)
            out[at_rows, lanes] = (source[:, lanes] / scale[:, lanes]).astype(out.dtype)

    for chunk in (*range(1, nchunk), 0):
        lo, hi = bounds[chunk]
        rounded(a_buf.at[lo:hi, :], 0, 0, chunk)
        if chunk:
            ring(0, 0, chunk).start()
            ring(1, 0, chunk).start()
        share(0, 0, chunk, c).start()
    for line in range(qd // LANES):
        scale_q[line:line + 1, :] = scale[:, line * LANES:(line + 1) * LANES]
    scale_k[...] = scale[:, qd:qd + kd]
    scale_v[...] = scale[:, qd + kd:]

    for hop in range(1, far + 1):
        for pair in zip(*(chunks(d, hop) for d in (0, 1))):
            for direction, chunk in enumerate(pair):
                if hop == 1 and chunk == 0:
                    for piece in range(early_rows // LOAD):
                        early_copy(direction, piece).wait_recv()
                    rounded(early.at[direction], direction, hop, chunk)
                else:
                    arrived(direction, hop, chunk).wait_recv()
                if hop + 1 <= far and chunk in chunks(direction, hop + 1):
                    ring(direction, hop, chunk).start()
                share(direction, hop, chunk, c).start()

        if hop == 1:
            @pl.when(is_root)
            def _():
                for i in range(nrows):
                    if i != ROOT:
                        tile_copy(i).wait_recv()
                for g in range(nrows // 2):
                    gains[w, 8 * g:8 * g + 8, :] = tiles[2 * g] + tiles[2 * g + 1]
                for i in range(1, nwidth):
                    gain_copy(i).start()
        if hop == 2:
            @pl.when(is_root)
            def _():
                for i in range(1, nwidth):
                    gain_copy(i).wait_recv()
                per = 2 * nwidth * small // LANES
                for g in range(nrows // 2):
                    full = gains[0, 8 * g:8 * g + 8, :]
                    for i in range(1, nwidth):
                        full = full + gains[i, 8 * g:8 * g + 8, :]
                    joined[g * per:(g + 1) * per, :] = full[:per, :]
                norm_out[...] = joined[...].astype(norm_out.dtype)
                for i in range(1, nrows):
                    norm_copy(i).start()

    for hop in range(far + 1):
        for direction in (0, 1) if hop else (0,):
            for chunk in chunks(direction, hop):
                share(direction, hop, chunk, 1 - c).wait_recv()
                share(direction, hop, chunk, c).wait_send()
    for hop in range(far):
        for direction in (0, 1):
            for chunk in chunks(direction, hop + 1):
                if hop or chunk:
                    ring(direction, hop, chunk).wait_send()
    for direction in (0, 1):
        for piece in range(early_rows // LOAD):
            early_copy(direction, piece).wait_send()
    for i in range(1, nrows):
        max_copy(i).wait_send()

    @pl.when(is_root)
    def _():
        for i in range(1, nwidth):
            gain_copy(i).wait_send()
        for i in range(1, nrows):
            norm_copy(i).wait_send()

    @pl.when(jnp.logical_not(is_root))
    def _():
        tile_copy(r).wait_send()
        norm_copy(1).wait_recv()


def write_kernel(dims, full, *refs):
    qd, kd = dims
    q, k, v = refs[4:7]
    sems = refs[-1]
    rows = full.shape[0]
    pieces = 8
    step = rows // pieces
    copies = []
    for i in range(pieces):
        span = pl.ds(i * step, step)
        copies.append((full.at[span, pl.ds(0, qd)], q.at[span, :]))
        copies.append((full.at[span, pl.ds(qd, kd)], k.at[span, :]))
        copies.append((full.at[span, pl.ds(qd + kd, kd)], v.at[span, :]))
    copies.extend(zip(refs[:4], refs[7:11]))
    started = [pltpu.make_async_copy(src, dst, sems.at[i]) for i, (src, dst) in enumerate(copies)]
    for copy in started:
        copy.start()
    for copy in started:
        copy.wait()


def shards(nrows, nwidth, one_q, other_q, one_k, other_k, one_v, other_v, mix, norm_t, norm_s):
    rows, qd = one_q.shape
    kd = one_k.shape[1]
    cols = qd + 2 * kd
    small = norm_t.shape[0]
    total = rows * nrows
    lines = small * nrows * nwidth // LANES
    far, nchunk = nrows // 4, len(bounds_of(rows))
    early_rows = bounds_of(rows)[0][1]
    dma = pltpu.SemaphoreType.DMA
    hbm = pl.BlockSpec(memory_space=pltpu.HBM)
    vmem = pl.BlockSpec(memory_space=pltpu.VMEM)
    full, scale_q, scale_k, scale_v, norm = pl.pallas_call(
        functools.partial(gather_kernel, nrows, nwidth, (rows, qd, kd)),
        out_shape=(
            pltpu.VMEM((total, cols), jnp.bfloat16),
            pltpu.VMEM((qd // LANES, LANES), jnp.float32),
            pltpu.VMEM((1, kd), jnp.float32),
            pltpu.VMEM((1, kd), jnp.float32),
            pltpu.VMEM((lines, LANES), jnp.bfloat16),
        ),
        in_specs=[hbm] * 9,
        out_specs=(vmem,) * 5,
        scratch_shapes=[
            pltpu.VMEM((1, rows), jnp.float32),
            pltpu.VMEM((1, small), jnp.float32),
            pltpu.VMEM((1, small), jnp.float32),
            pltpu.VMEM((rows, cols), jnp.float32),
            pltpu.VMEM((rows, cols), jnp.float32),
            pltpu.VMEM((2, early_rows, cols), jnp.float32),
            pltpu.VMEM((rows, LANES), jnp.float32),
            pltpu.VMEM((8, cols), jnp.float32),
            pltpu.VMEM((nrows, 1, cols), jnp.float32),
            pltpu.VMEM((8, LANES), jnp.float32),
            pltpu.VMEM((nrows, 8, LANES), jnp.float32),
            pltpu.VMEM((nwidth, 4 * nrows, LANES), jnp.float32),
            pltpu.VMEM((lines, LANES), jnp.float32),
            pltpu.SemaphoreType.REGULAR((2, far + 1)),
            dma((3,)),
            dma((rows // LOAD, 6)),
            dma((nrows,)),
            dma((nrows,)),
            dma(()),
            dma((nrows,)),
            dma((nwidth,)),
            dma((nwidth,)),
            dma((nrows,)),
            dma(()),
            dma((2, early_rows // LOAD)),
            dma((2, early_rows // LOAD)),
            dma((2, far, nchunk)),
            dma((2, far, nchunk)),
            dma((2, far + 1, nchunk)),
            dma((2, far + 1, nchunk)),
        ],
        compiler_params=pltpu.CompilerParams(
            collective_id=0, has_side_effects=True, vmem_limit_bytes=24 * 1024 * 1024),
        name="gather",
    )(*(pltpu.with_memory_space_constraint(x, pltpu.HBM) for x in (
        one_q, other_q, one_k, other_k, one_v, other_v,
        mix.reshape(1, -1), norm_t.reshape(1, -1), norm_s.reshape(1, -1))))
    q, k, v, scale_q, scale_k, scale_v, norm_o = pl.pallas_call(
        functools.partial(write_kernel, (qd, kd)),
        out_shape=(
            jax.ShapeDtypeStruct((total, qd), jnp.bfloat16),
            jax.ShapeDtypeStruct((total, kd), jnp.bfloat16),
            jax.ShapeDtypeStruct((total, kd), jnp.bfloat16),
            jax.ShapeDtypeStruct((qd // LANES, LANES), jnp.float32),
            jax.ShapeDtypeStruct((1, kd), jnp.float32),
            jax.ShapeDtypeStruct((1, kd), jnp.float32),
            jax.ShapeDtypeStruct((lines, LANES), jnp.bfloat16),
        ),
        in_specs=[vmem] * 5,
        out_specs=(hbm,) * 7,
        scratch_shapes=[pltpu.SemaphoreType.DMA((28,))],
        compiler_params=pltpu.CompilerParams(vmem_limit_bytes=1024 * 1024),
        name="write",
    )(full, scale_q, scale_k, scale_v, norm)
    return (q, k, v, scale_q.reshape(-1), scale_k.reshape(-1), scale_v.reshape(-1),
            norm_o.reshape(-1))


def solution(mesh):
    rows = ("site", "rows")
    return jax.shard_map(
        functools.partial(shards, mesh.shape["rows"], mesh.shape["width"]),
        mesh=mesh,
        in_specs=(P(rows, "width"),) * 6 + (P(rows), P(("site", "rows", "width")), P(("site", "rows", "width"))),
        out_specs=(P("site", "width"),) * 3 + (P(("site", "width")),) * 3 + (P("site"),),
        check_vma=False,
    )
```

time: 108 us -> 109 us (level)
  no operation moved by 1% of the time
where the time goes in v2:
time: 109 us; the launch traced here: 108 us
  Pallas kernels  108 us (99%)
    pallas_call x1, Pallas kernels, shards(): pl.pallas_call(functools.partial(gather_kernel, nrows, nwidth, (rows, qd,...  102 us
    pallas_call x1, Pallas kernels, shards(): pl.pallas_call(functools.partial(write_kernel, (qd, kd)), out_shape=(jax....  6.01 us

profile of v2, /device:TPU:1, one launch (start us, length us, event | category | flops | bytes accessed | tf_op | source)
XLA Modules:
  0.0 108.5 jit_solution(796904929845951581)
XLA Ops:
  0.6 101.8 %gather.1 = (bf16[7168,1152]{1,0:T(8,128)(2,1)S(1)}, f32[7,128]{1,0:T(8,128)S(1)}, f32[1,128]{1,0:T(1,128)S(1)}, f32[1,128]{1,0:T(1,128)S(1)}, bf16[56,128]{1,0:T(8,128)(2,1)S(1)}) custom-call(f32[448,896]{1,0:T(8,128)} %refs_0_.1, f32[448,896]{1,0:T(8,128)} %refs_1_.1, f32[448,128]{1,0:T(8,128)} %refs_2_.1, f32[448,128]{1,0:T(8,128)} %refs_3_.1, ...), custom_call_target="tpu_custom_call" | custom-call | tf_op jit(solution)/shard_map/gather/pallas_call | solution.py:322
  102.5 6.0 %write.1 = (bf16[7168,896]{1,0:T(8,128)(2,1)}, bf16[7168,128]{1,0:T(8,128)(2,1)}, bf16[7168,128]{1,0:T(8,128)(2,1)}, f32[7,128]{1,0:T(8,128)}, f32[1,128]{1,0:T(...) custom-call(bf16[7168,1152]{1,0:T(8,128)(2,1)S(1)} %get-tuple-element.19.full, ...), custom_call_target="tpu_custom_call" | custom-call | tf_op jit(solution)/shard_map/write/pallas_call | solution.py:371

commit v3 on v2

v3 whole, which is shorter than its diff:
```python
import functools

import jax
import jax.numpy as jnp
from jax import lax
from jax.experimental import pallas as pl
from jax.experimental.pallas import tpu as pltpu
from jax.sharding import PartitionSpec as P

MESH = pl.DeviceIdType.MESH
LANES = 128
LOAD = 112
ROOT = 1
EARLY = 1
CUT = 48


def bounds_of(rows):
    half = rows // 2
    cuts = [0, CUT, half]
    cuts += [half + at for at in cuts[1:]]
    return list(zip(cuts, cuts[1:]))


def gather_kernel(nrows, nwidth, dims, *refs):
    (one_q, other_q, one_k, other_k, one_v, other_v, mix_hbm, norm_t_hbm, norm_s_hbm,
     out, scale_q, scale_k, scale_v, norm_out,
     mix, norm_t, norm_s, a_buf, b_buf, early, mixb, acc, maxima, seg, tiles, gains, joined,
     lead_sem, in_sem, max_send, max_recv, tile_send, tile_recv, gain_send, gain_recv, norm_send, norm_recv,
     early_send, early_recv, ring_send, ring_recv, share_send, share_recv) = refs
    rows, qd, kd = dims
    cols = qd + 2 * kd
    nz = nrows // 2
    far = nz // 2
    r = lax.axis_index("rows")
    w = lax.axis_index("width")
    z, c = r // 2, lax.rem(r, 2)
    bounds = bounds_of(rows)
    nchunk = len(bounds)
    is_root = r == ROOT

    def row_peer(i):
        return {"rows": lax.rem(r + i, nrows)}

    def width_peer(i):
        return {"width": lax.rem(w + i, nwidth)}

    ahead = (row_peer(2), row_peer(nrows - 2))
    partner = {"rows": r + 1 - 2 * c}
    farthest_first = sorted(range(1, nrows), key=lambda i: -min(i, nrows - i))

    barrier = pltpu.get_barrier_semaphore()
    for i in farthest_first:
        pl.semaphore_signal(barrier, inc=1, device_id=row_peer(i), device_id_type=MESH)

    @pl.when(is_root)
    def _():
        for i in range(1, nwidth):
            pl.semaphore_signal(barrier, inc=1, device_id=width_peer(i), device_id_type=MESH)

    leads = [
        pltpu.make_async_copy(src, dst, lead_sem.at[i])
        for i, (src, dst) in enumerate(((mix_hbm, mix), (norm_t_hbm, norm_t), (norm_s_hbm, norm_s)))
    ]
    for copy in leads:
        copy.start(priority=1)
    parts = (
        (one_q, a_buf, 0, qd), (other_q, b_buf, 0, qd),
        (one_k, a_buf, qd, kd), (other_k, b_buf, qd, kd),
        (one_v, a_buf, qd + kd, kd), (other_v, b_buf, qd + kd, kd),
    )

    def loads(step):
        span = pl.ds(step * LOAD, LOAD)
        return [
            pltpu.make_async_copy(src.at[span, :], dst.at[span, pl.ds(at, n)], in_sem.at[step])
            for src, dst, at, n in parts
        ]

    for step in range(rows // LOAD):
        for copy in loads(step):
            copy.start()
    for copy in leads:
        copy.wait()

    for at in range(0, rows, LANES):
        n = min(LANES, rows - at)
        line = mix[:, at:at + n]
        if n < LANES:
            line = jnp.concatenate([line, jnp.zeros((1, LANES - n), jnp.float32)], axis=1)
        square = jnp.transpose(jnp.broadcast_to(line, (LANES, LANES)))
        mixb[at:at + n, :] = square[:n, :]

    acc[...] = jnp.zeros((8, cols), jnp.float32)
    for step in range(rows // LOAD):
        both = a_buf.at[pl.ds(0, 2 * LOAD), :]
        pltpu.make_async_copy(both, both, in_sem.at[step]).wait()
        span = slice(step * LOAD, (step + 1) * LOAD)
        m = mixb[span, :]
        rest = 1.0 - m
        for at in range(0, cols, LANES):
            lanes = slice(at, at + LANES)
            whole = m * a_buf[span, lanes] + rest * b_buf[span, lanes]
            a_buf[span, lanes] = whole
            top = jnp.max(jnp.abs(whole).reshape(LOAD // 8, 8, LANES), axis=0)
            acc[:, lanes] = jnp.maximum(acc[:, lanes], top)
    maxima[r] = jnp.max(acc[...], axis=0, keepdims=True)

    pl.semaphore_wait(barrier, nrows - 1 + jnp.where(is_root, nwidth - 1, 0))

    def max_copy(i):
        return pltpu.make_async_remote_copy(
            src_ref=maxima.at[r], dst_ref=maxima.at[r], send_sem=max_send, recv_sem=max_recv,
            device_id=row_peer(i), device_id_type=MESH)

    def all_of(ref, count, send_sem, recv_sem):
        part = ref.at[pl.ds(0, count)]
        return pltpu.make_async_remote_copy(
            src_ref=part, dst_ref=part, send_sem=send_sem, recv_sem=recv_sem, device_id=partner, device_id_type=MESH)

    for i in farthest_first:
        max_copy(i).start()

    def early_copy(direction, chunk):
        span = pl.ds(bounds[chunk][0], bounds[chunk][1] - bounds[chunk][0])
        return pltpu.make_async_remote_copy(
            src_ref=a_buf.at[span, :], dst_ref=early.at[direction, span, :], send_sem=early_send,
            recv_sem=early_recv.at[direction, chunk], device_id=ahead[direction], device_id_type=MESH)

    for chunk in range(EARLY):
        for direction in (0, 1):
            early_copy(direction, chunk).start()

    small = norm_t.shape[1]
    pos = lax.rem(r, 2) * nwidth + w
    first, lane0 = (pos * small) // LANES, lax.rem(pos * small, LANES)
    seg[...] = jnp.zeros((8, LANES), jnp.float32)
    seg[0:1, 0:small] = norm_t[...] + norm_s[...]
    turned = pltpu.roll(seg[...], lane0, 1)[0:1, :]
    lane = lax.broadcasted_iota(jnp.int32, (8, LANES), 1)
    line = lax.broadcasted_iota(jnp.int32, (8, LANES), 0)
    here = ((line == first) & (lane >= lane0)) | ((line == first + 1) & (lane < lane0))
    tiles[r] = jnp.where(here, jnp.broadcast_to(turned, (8, LANES)), 0.0)

    def tile_copy(source):
        return pltpu.make_async_remote_copy(
            src_ref=tiles.at[source], dst_ref=tiles.at[source], send_sem=tile_send, recv_sem=tile_recv,
            device_id={"rows": ROOT}, device_id_type=MESH)

    def gain_copy(i):
        return pltpu.make_async_remote_copy(
            src_ref=gains.at[w], dst_ref=gains.at[w], send_sem=gain_send, recv_sem=gain_recv,
            device_id=width_peer(i), device_id_type=MESH)

    def norm_copy(i):
        return pltpu.make_async_remote_copy(
            src_ref=norm_out, dst_ref=norm_out, send_sem=norm_send, recv_sem=norm_recv,
            device_id=row_peer(i), device_id_type=MESH)

    @pl.when(jnp.logical_not(is_root))
    def _():
        tile_copy(r).start()

    all_of(maxima, nrows - 1, max_send, max_recv).wait_recv()
    scale = maxima[0]
    for i in range(1, nrows):
        scale = jnp.maximum(scale, maxima[i])

    def place(direction, hop, chunk):
        lo, hi = bounds[chunk]
        owner = lax.rem(z - hop + nz, nz) if direction == 0 else lax.rem(z + hop, nz)
        return pl.ds(pl.multiple_of((owner * 2 + c) * rows + lo, 16), hi - lo)

    def landing(direction, hop, chunk):
        return (2 * hop + direction) * nchunk + chunk if hop + 1 < far else 2 * hop * nchunk + chunk

    def ring(direction, hop, chunk):
        ref = out.at[place(direction, hop, chunk), :]
        return pltpu.make_async_remote_copy(
            src_ref=ref, dst_ref=ref, send_sem=ring_send, recv_sem=ring_recv.at[landing(direction, hop, chunk)],
            device_id=ahead[direction], device_id_type=MESH)

    def arrived(direction, hop, chunk):
        ref = out.at[place(direction, hop, chunk), :]
        return pltpu.make_async_remote_copy(
            src_ref=ref, dst_ref=ref, send_sem=ring_send, recv_sem=ring_recv.at[landing(direction, hop - 1, chunk)],
            device_id=ahead[direction], device_id_type=MESH)

    def share(direction, hop, chunk):
        ref = out.at[place(direction, hop, chunk), :]
        return pltpu.make_async_remote_copy(
            src_ref=ref, dst_ref=ref, send_sem=share_send, recv_sem=share_recv,
            device_id=partner, device_id_type=MESH)

    def chunks(direction, hop):
        if hop < far:
            return [0, 1, 3, 2] if hop == 1 else [1, 0, 3, 2]
        return [1, 0] if direction == 0 else [3, 2]

    def rounded(source, direction, hop, chunk):
        at_rows = place(direction, hop, chunk)
        for at in range(0, cols, LANES):
            lanes = slice(at, at + LANES)
            out[at_rows, lanes] = (source[:, lanes] / scale[:, lanes]).astype(out.dtype)

    for chunk in (1, 3, 2, 0):
        lo, hi = bounds[chunk]
        rounded(a_buf.at[lo:hi, :], 0, 0, chunk)
        if chunk >= EARLY:
            for direction in (0, 1):
                ring(direction, 0, chunk).start()
        share(0, 0, chunk).start()
    for line in range(qd // LANES):
        scale_q[line:line + 1, :] = scale[:, line * LANES:(line + 1) * LANES]
    scale_k[...] = scale[:, qd:qd + kd]
    scale_v[...] = scale[:, qd + kd:]

    for hop in range(1, far + 1):
        for step in zip(*(chunks(d, hop) for d in (0, 1))):
            for direction, chunk in enumerate(step):
                if hop == 1 and chunk < EARLY:
                    early_copy(direction, chunk).wait_recv()
                    rounded(early.at[direction, bounds[chunk][0]:bounds[chunk][1], :], direction, hop, chunk)
                else:
                    arrived(direction, hop, chunk).wait_recv()
                if hop + 1 <= far and chunk in chunks(direction, hop + 1):
                    ring(direction, hop, chunk).start()
                share(direction, hop, chunk).start()

        if hop == 1:
            @pl.when(is_root)
            def _():
                all_of(tiles, nrows - 1, tile_send, tile_recv).wait_recv()
                for g in range(nrows // 2):
                    gains[w, 8 * g:8 * g + 8, :] = tiles[2 * g] + tiles[2 * g + 1]
                for i in range(1, nwidth):
                    gain_copy(i).start()
        if hop == 2:
            @pl.when(is_root)
            def _():
                all_of(gains, nwidth - 1, gain_send, gain_recv).wait_recv()
                per = 2 * nwidth * small // LANES
                for g in range(nrows // 2):
                    full = gains[0, 8 * g:8 * g + 8, :]
                    for i in range(1, nwidth):
                        full = full + gains[i, 8 * g:8 * g + 8, :]
                    joined[g * per:(g + 1) * per, :] = full[:per, :]
                norm_out[...] = joined[...].astype(norm_out.dtype)
                for i in range(1, nrows):
                    norm_copy(i).start()

    all_of(out, nz * rows, share_send, share_recv).wait_recv()
    all_of(out, nz * rows, share_send, share_recv).wait_send()
    all_of(out, (nz - 1) * rows - 2 * bounds[EARLY - 1][1], ring_send, ring_recv.at[0]).wait_send()
    for chunk in range(EARLY):
        for direction in (0, 1):
            early_copy(direction, chunk).wait_send()
    all_of(maxima, nrows - 1, max_send, max_recv).wait_send()

    @pl.when(is_root)
    def _():
        all_of(gains, nwidth - 1, gain_send, gain_recv).wait_send()
        for i in range(1, nrows):
            norm_copy(i).wait_send()

    @pl.when(jnp.logical_not(is_root))
    def _():
        tile_copy(r).wait_send()
        norm_copy(1).wait_recv()


def write_kernel(dims, full, *refs):
    qd, kd = dims
    q, k, v = refs[4:7]
    sems = refs[-1]
    half = full.shape[0] // 2
    started = []
    for i in range(2):
        span = pl.ds(i * half, half)
        for j, (o, at, n) in enumerate(((q, 0, qd), (k, qd, kd), (v, qd + kd, kd))):
            started.append((i, pltpu.make_async_copy(full.at[span, pl.ds(at, n)], o.at[span, :], sems.at[4 + 3 * i + j])))
    started += [(1, pltpu.make_async_copy(src, dst, sems.at[i])) for i, (src, dst) in enumerate(zip(refs[:4], refs[7:11]))]
    for i, copy in started:
        copy.start(priority=i)
    for i, copy in started:
        copy.wait()


def shards(nrows, nwidth, one_q, other_q, one_k, other_k, one_v, other_v, mix, norm_t, norm_s):
    rows, qd = one_q.shape
    kd = one_k.shape[1]
    cols = qd + 2 * kd
    small = norm_t.shape[0]
    total = rows * nrows
    lines = small * nrows * nwidth // LANES
    far, nchunk = nrows // 4, len(bounds_of(rows))
    early_rows = bounds_of(rows)[EARLY - 1][1]
    dma = pltpu.SemaphoreType.DMA
    hbm = pl.BlockSpec(memory_space=pltpu.HBM)
    vmem = pl.BlockSpec(memory_space=pltpu.VMEM)
    full, scale_q, scale_k, scale_v, norm = pl.pallas_call(
        functools.partial(gather_kernel, nrows, nwidth, (rows, qd, kd)),
        out_shape=(
            pltpu.VMEM((total, cols), jnp.bfloat16),
            pltpu.VMEM((qd // LANES, LANES), jnp.float32),
            pltpu.VMEM((1, kd), jnp.float32),
            pltpu.VMEM((1, kd), jnp.float32),
            pltpu.VMEM((lines, LANES), jnp.bfloat16),
        ),
        in_specs=[hbm] * 9,
        out_specs=(vmem,) * 5,
        scratch_shapes=[
            pltpu.VMEM((1, rows), jnp.float32),
            pltpu.VMEM((1, small), jnp.float32),
            pltpu.VMEM((1, small), jnp.float32),
            pltpu.VMEM((rows, cols), jnp.float32),
            pltpu.VMEM((rows, cols), jnp.float32),
            pltpu.VMEM((2, early_rows, cols), jnp.float32),
            pltpu.VMEM((rows, LANES), jnp.float32),
            pltpu.VMEM((8, cols), jnp.float32),
            pltpu.VMEM((nrows, 1, cols), jnp.float32),
            pltpu.VMEM((8, LANES), jnp.float32),
            pltpu.VMEM((nrows, 8, LANES), jnp.float32),
            pltpu.VMEM((nwidth, 4 * nrows, LANES), jnp.float32),
            pltpu.VMEM((lines, LANES), jnp.float32),
            dma((3,)),
            dma((rows // LOAD,)),
            dma(()),
            dma(()),
            dma(()),
            dma(()),
            dma(()),
            dma(()),
            dma(()),
            dma(()),
            dma(()),
            dma((2, EARLY)),
            dma(()),
            dma((2 * (far - 1) * nchunk + nchunk,)),
            dma(()),
            dma(()),
        ],
        compiler_params=pltpu.CompilerParams(
            collective_id=0, has_side_effects=True, vmem_limit_bytes=24 * 1024 * 1024),
        name="gather",
    )(*(pltpu.with_memory_space_constraint(x, pltpu.HBM) for x in (
        one_q, other_q, one_k, other_k, one_v, other_v,
        mix.reshape(1, -1), norm_t.reshape(1, -1), norm_s.reshape(1, -1))))
    q, k, v, scale_q, scale_k, scale_v, norm_o = pl.pallas_call(
        functools.partial(write_kernel, (qd, kd)),
        out_shape=(
            jax.ShapeDtypeStruct((total, qd), jnp.bfloat16),
            jax.ShapeDtypeStruct((total, kd), jnp.bfloat16),
            jax.ShapeDtypeStruct((total, kd), jnp.bfloat16),
            jax.ShapeDtypeStruct((qd // LANES, LANES), jnp.float32),
            jax.ShapeDtypeStruct((1, kd), jnp.float32),
            jax.ShapeDtypeStruct((1, kd), jnp.float32),
            jax.ShapeDtypeStruct((lines, LANES), jnp.bfloat16),
        ),
        in_specs=[vmem] * 5,
        out_specs=(hbm,) * 7,
        scratch_shapes=[dma((10,))],
        compiler_params=pltpu.CompilerParams(vmem_limit_bytes=1024 * 1024),
        name="write",
    )(full, scale_q, scale_k, scale_v, norm)
    return (q, k, v, scale_q.reshape(-1), scale_k.reshape(-1), scale_v.reshape(-1),
            norm_o.reshape(-1))


def solution(mesh):
    rows = ("site", "rows")
    return jax.shard_map(
        functools.partial(shards, mesh.shape["rows"], mesh.shape["width"]),
        mesh=mesh,
        in_specs=(P(rows, "width"),) * 6 + (P(rows), P(("site", "rows", "width")), P(("site", "rows", "width"))),
        out_specs=(P("site", "width"),) * 3 + (P(("site", "width")),) * 3 + (P("site"),),
        check_vma=False,
    )
```

time: 109 us -> 101 us (0.927)
  Pallas kernels: 108 us -> 99.9 us
    pallas_call x1, Pallas kernels: 102 us -> 94 us  [shards(): pl.pallas_call(functools.partial(gather_kernel, nrows, nwidth, (rows, qd,...]
where the time goes in v3:
time: 101 us
  Pallas kernels  99.9 us (99%)
    pallas_call x1, Pallas kernels, shards(): pl.pallas_call(functools.partial(gather_kernel, nrows, nwidth, (rows, qd,...  94 us
    pallas_call x1, Pallas kernels, shards(): pl.pallas_call(functools.partial(write_kernel, (qd, kd)), out_shape=(jax....  5.9 us

profile of v3, /device:TPU:1, one launch (start us, length us, event | category | flops | bytes accessed | tf_op | source)
XLA Modules:
  0.0 100.5 jit_solution(5184585091340126049)
XLA Ops:
  0.6 94.0 %gather.1 = (bf16[7168,1152]{1,0:T(8,128)(2,1)S(1)}, f32[7,128]{1,0:T(8,128)S(1)}, f32[1,128]{1,0:T(1,128)S(1)}, f32[1,128]{1,0:T(1,128)S(1)}, bf16[56,128]{1,0:T(8,128)(2,1)S(1)}) custom-call(f32[448,896]{1,0:T(8,128)} %refs_0_.1, f32[448,896]{1,0:T(8,128)} %refs_1_.1, f32[448,128]{1,0:T(8,128)} %refs_2_.1, f32[448,128]{1,0:T(8,128)} %refs_3_.1, ...), custom_call_target="tpu_custom_call" | custom-call | tf_op jit(solution)/shard_map/gather/pallas_call | solution.py:301
  94.6 5.9 %write.1 = (bf16[7168,896]{1,0:T(8,128)(2,1)}, bf16[7168,128]{1,0:T(8,128)(2,1)}, bf16[7168,128]{1,0:T(8,128)(2,1)}, f32[7,128]{1,0:T(8,128)}, f32[1,128]{1,0:T(...) custom-call(bf16[7168,1152]{1,0:T(8,128)(2,1)S(1)} %get-tuple-element.19.full, ...), custom_call_target="tpu_custom_call" | custom-call | tf_op jit(solution)/shard_map/write/pallas_call | solution.py:349

commit v4 on v3

--- a/solution.py
+++ b/solution.py
@@ -9,15 +9,15 @@
 
 MESH = pl.DeviceIdType.MESH
 LANES = 128
-LOAD = 112
-ROOT = 1
-EARLY = 1
-CUT = 48
+LOAD = 64
+EARLY = 4
+CUTS = (64, 112, 192)
+TINY = 1e-30
 
 
 def bounds_of(rows):
     half = rows // 2
-    cuts = [0, CUT, half]
+    cuts = [0, *CUTS, half]
     cuts += [half + at for at in cuts[1:]]
     return list(zip(cuts, cuts[1:]))
 
@@ -25,8 +25,8 @@
 def gather_kernel(nrows, nwidth, dims, *refs):
     (one_q, other_q, one_k, other_k, one_v, other_v, mix_hbm, norm_t_hbm, norm_s_hbm,
      out, scale_q, scale_k, scale_v, norm_out,
-     mix, norm_t, norm_s, a_buf, b_buf, early, mixb, acc, maxima, seg, tiles, gains, joined,
-     lead_sem, in_sem, max_send, max_recv, tile_send, tile_recv, gain_send, gain_recv, norm_send, norm_recv,
+     mix, norm_t, norm_s, a_buf, b_buf, early, mixb, acc, firsts, pair, maxima, seg, tiles, gains, joined,
+     tokens, lead_sem, in_sem, first_send, first_recv, pair_send, pair_recv, max_send, max_recv, tile_send, tile_recv, gain_send, gain_recv, norm_send, norm_recv,
      early_send, early_recv, ring_send, ring_recv, share_send, share_recv) = refs
     rows, qd, kd = dims
     cols = qd + 2 * kd
@@ -37,7 +37,8 @@
     z, c = r // 2, lax.rem(r, 2)
     bounds = bounds_of(rows)
     nchunk = len(bounds)
-    is_root = r == ROOT
+    root = nrows // 2 + 1
+    is_root = r == root
 
     def row_peer(i):
         return {"rows": lax.rem(r + i, nrows)}
@@ -47,11 +48,14 @@
 
     ahead = (row_peer(2), row_peer(nrows - 2))
     partner = {"rows": r + 1 - 2 * c}
-    farthest_first = sorted(range(1, nrows), key=lambda i: -min(i, nrows - i))
+    farthest_first = sorted(range(1, nz), key=lambda i: -min(i, nz - i))
 
     barrier = pltpu.get_barrier_semaphore()
-    for i in farthest_first:
-        pl.semaphore_signal(barrier, inc=1, device_id=row_peer(i), device_id_type=MESH)
+    for dz in (1, nz - 1):
+        for core in (0, 1):
+            pl.semaphore_signal(
+                barrier, inc=1, device_id={"rows": lax.rem(z + dz, nz) * 2 + core}, device_id_type=MESH)
+    pl.semaphore_signal(barrier, inc=1, device_id=partner, device_id_type=MESH)
 
     @pl.when(is_root)
     def _():
@@ -77,13 +81,11 @@
             for src, dst, at, n in parts
         ]
 
-    for step in range(rows // LOAD):
-        for copy in loads(step):
-            copy.start()
-    for copy in leads:
-        copy.wait()
-
-    for at in range(0, rows, LANES):
+    def wait_load(step):
+        both = a_buf.at[pl.ds(0, 2 * LOAD), :]
+        pltpu.make_async_copy(both, both, in_sem.at[step]).wait()
+
+    def spread(at):
         n = min(LANES, rows - at)
         line = mix[:, at:at + n]
         if n < LANES:
@@ -91,10 +93,7 @@
         square = jnp.transpose(jnp.broadcast_to(line, (LANES, LANES)))
         mixb[at:at + n, :] = square[:n, :]
 
-    acc[...] = jnp.zeros((8, cols), jnp.float32)
-    for step in range(rows // LOAD):
-        both = a_buf.at[pl.ds(0, 2 * LOAD), :]
-        pltpu.make_async_copy(both, both, in_sem.at[step]).wait()
+    def mixed(step):
         span = slice(step * LOAD, (step + 1) * LOAD)
         m = mixb[span, :]
         rest = 1.0 - m
@@ -103,15 +102,90 @@
             whole = m * a_buf[span, lanes] + rest * b_buf[span, lanes]
             a_buf[span, lanes] = whole
             top = jnp.max(jnp.abs(whole).reshape(LOAD // 8, 8, LANES), axis=0)
-            acc[:, lanes] = jnp.maximum(acc[:, lanes], top)
-    maxima[r] = jnp.max(acc[...], axis=0, keepdims=True)
-
-    pl.semaphore_wait(barrier, nrows - 1 + jnp.where(is_root, nwidth - 1, 0))
+            acc[:, lanes] = top if step == 0 else jnp.maximum(acc[:, lanes], top)
+
+    def coded(chunk, own):
+        inverse = 1.0 / jnp.maximum(own, TINY)
+        span = slice(*bounds[chunk])
+        for at in range(0, cols, LANES):
+            lanes = slice(at, at + LANES)
+            v = a_buf[span, lanes] * inverse[:, lanes]
+            v2 = v * v
+            v4 = v2 * v2
+            v8 = v4 * v4 * 2.0**63
+            code = v8 * v8
+            early[2, span, lanes] = jnp.where(v < 0.0, -code, code).astype(early.dtype)
+
+    def early_copy(direction, chunk):
+        span = pl.ds(bounds[chunk][0], bounds[chunk][1] - bounds[chunk][0])
+        return pltpu.make_async_remote_copy(
+            src_ref=early.at[2, span, :], dst_ref=early.at[direction, span, :], send_sem=early_send,
+            recv_sem=early_recv.at[direction, chunk], device_id=ahead[direction], device_id_type=MESH)
+
+    def first_copy(direction, part):
+        return pltpu.make_async_remote_copy(
+            src_ref=firsts.at[2, part], dst_ref=firsts.at[direction, part], send_sem=first_send,
+            recv_sem=first_recv.at[direction, part], device_id=ahead[direction], device_id_type=MESH)
+
+    for copy in loads(0):
+        copy.start()
+    for copy in leads:
+        copy.wait()
+    wait_load(0)
+    for step in range(1, rows // LOAD):
+        for copy in loads(step):
+            copy.start()
+    spread(0)
+    mixed(0)
+    firsts[2, 0] = jnp.max(acc[...], axis=0, keepdims=True)
+    coded(0, firsts[2, 0])
+
+    pl.semaphore_wait(barrier, 5 + jnp.where(is_root, nwidth - 1, 0))
+    for direction in (0, 1):
+        early_copy(direction, 0).start()
+
+    def tell(direction, hop):
+        pl.semaphore_signal(tokens.at[direction, hop - 2], inc=1, device_id=ahead[direction], device_id_type=MESH)
+
+    def heard(hop):
+        for direction in (0, 1) if hop < far else (0,):
+            pl.semaphore_wait(tokens.at[direction, hop - 2], 1)
+            if hop + 1 < far or (hop < far and direction == 0):
+                tell(direction, hop + 1)
+
+    for direction in (0, 1) if far > 2 else (0,):
+        tell(direction, 2)
+    for direction in (0, 1):
+        first_copy(direction, 0).start()
+    heard(2)
+
+    for at in range(LANES, rows, LANES):
+        spread(at)
+    for step in range(1, rows // LOAD):
+        wait_load(step)
+        mixed(step)
+
+    def pair_copy(core):
+        return pltpu.make_async_remote_copy(
+            src_ref=pair.at[core], dst_ref=pair.at[core], send_sem=pair_send, recv_sem=pair_recv,
+            device_id=partner, device_id_type=MESH)
+
+    firsts[2, 1] = jnp.max(acc[...], axis=0, keepdims=True)
+    pair[c] = firsts[2, 1]
+    pair_copy(c).start()
+    coded(1, firsts[2, 1])
+    for direction in (0, 1):
+        first_copy(direction, 1).start()
+        early_copy(direction, 1).start()
+    for hop in range(3, far + 1):
+        heard(hop)
+    pair_copy(1 - c).wait_recv()
+    maxima[z] = jnp.maximum(pair[0], pair[1])
 
     def max_copy(i):
         return pltpu.make_async_remote_copy(
-            src_ref=maxima.at[r], dst_ref=maxima.at[r], send_sem=max_send, recv_sem=max_recv,
-            device_id=row_peer(i), device_id_type=MESH)
+            src_ref=maxima.at[z], dst_ref=maxima.at[z], send_sem=max_send, recv_sem=max_recv,
+            device_id=row_peer(2 * i), device_id_type=MESH)
 
     def all_of(ref, count, send_sem, recv_sem):
         part = ref.at[pl.ds(0, count)]
@@ -120,14 +194,8 @@
 
     for i in farthest_first:
         max_copy(i).start()
-
-    def early_copy(direction, chunk):
-        span = pl.ds(bounds[chunk][0], bounds[chunk][1] - bounds[chunk][0])
-        return pltpu.make_async_remote_copy(
-            src_ref=a_buf.at[span, :], dst_ref=early.at[direction, span, :], send_sem=early_send,
-            recv_sem=early_recv.at[direction, chunk], device_id=ahead[direction], device_id_type=MESH)
-
-    for chunk in range(EARLY):
+    for chunk in range(2, EARLY):
+        coded(chunk, firsts[2, 1])
         for direction in (0, 1):
             early_copy(direction, chunk).start()
 
@@ -145,7 +213,7 @@
     def tile_copy(source):
         return pltpu.make_async_remote_copy(
             src_ref=tiles.at[source], dst_ref=tiles.at[source], send_sem=tile_send, recv_sem=tile_recv,
-            device_id={"rows": ROOT}, device_id_type=MESH)
+            device_id={"rows": root}, device_id_type=MESH)
 
     def gain_copy(i):
         return pltpu.make_async_remote_copy(
@@ -161,9 +229,9 @@
     def _():
         tile_copy(r).start()
 
-    all_of(maxima, nrows - 1, max_send, max_recv).wait_recv()
+    all_of(maxima, nz - 1, max_send, max_recv).wait_recv()
     scale = maxima[0]
-    for i in range(1, nrows):
+    for i in range(1, nz):
         scale = jnp.maximum(scale, maxima[i])
 
     def place(direction, hop, chunk):
@@ -171,20 +239,19 @@
         owner = lax.rem(z - hop + nz, nz) if direction == 0 else lax.rem(z + hop, nz)
         return pl.ds(pl.multiple_of((owner * 2 + c) * rows + lo, 16), hi - lo)
 
-    def landing(direction, hop, chunk):
-        return (2 * hop + direction) * nchunk + chunk if hop + 1 < far else 2 * hop * nchunk + chunk
+    def landing(hop, chunk):
+        return hop * nchunk + chunk - EARLY
 
     def ring(direction, hop, chunk):
         ref = out.at[place(direction, hop, chunk), :]
         return pltpu.make_async_remote_copy(
-            src_ref=ref, dst_ref=ref, send_sem=ring_send, recv_sem=ring_recv.at[landing(direction, hop, chunk)],
+            src_ref=ref, dst_ref=ref, send_sem=ring_send, recv_sem=ring_recv.at[landing(hop, chunk)],
             device_id=ahead[direction], device_id_type=MESH)
 
-    def arrived(direction, hop, chunk):
-        ref = out.at[place(direction, hop, chunk), :]
-        return pltpu.make_async_remote_copy(
-            src_ref=ref, dst_ref=ref, send_sem=ring_send, recv_sem=ring_recv.at[landing(direction, hop - 1, chunk)],
-            device_id=ahead[direction], device_id_type=MESH)
+    def arrived(hop, chunk):
+        lo, hi = bounds[chunk]
+        sides = 2 if hop < far else 1
+        all_of(out, sides * (hi - lo), ring_send, ring_recv.at[landing(hop - 1, chunk)]).wait_recv()
 
     def share(direction, hop, chunk):
         ref = out.at[place(direction, hop, chunk), :]
@@ -194,8 +261,8 @@
 
     def chunks(direction, hop):
         if hop < far:
-            return [0, 1, 3, 2] if hop == 1 else [1, 0, 3, 2]
-        return [1, 0] if direction == 0 else [3, 2]
+            return list(range(nchunk))
+        return list(range(nchunk // 2)) if direction == 0 else list(range(nchunk // 2, nchunk))
 
     def rounded(source, direction, hop, chunk):
         at_rows = place(direction, hop, chunk)
@@ -203,7 +270,19 @@
             lanes = slice(at, at + LANES)
             out[at_rows, lanes] = (source[:, lanes] / scale[:, lanes]).astype(out.dtype)
 
-    for chunk in (1, 3, 2, 0):
+    def decoded(direction, chunk):
+        part = min(chunk, 1)
+        if chunk < 2:
+            first_copy(direction, part).wait_recv()
+        factor = jnp.maximum(firsts[direction, part], TINY) / scale
+        at_rows = place(direction, 1, chunk)
+        for at in range(0, cols, LANES):
+            lanes = slice(at, at + LANES)
+            code = early[direction, bounds[chunk][0]:bounds[chunk][1], lanes].astype(jnp.float32)
+            size = jnp.exp2(jnp.log2(jnp.abs(code)) * (1.0 / 16.0) - 126.0 / 16.0)
+            out[at_rows, lanes] = (jnp.where(code < 0.0, -size, size) * factor[:, lanes]).astype(out.dtype)
+
+    for chunk in (*range(EARLY, nchunk), *range(EARLY)):
         lo, hi = bounds[chunk]
         rounded(a_buf.at[lo:hi, :], 0, 0, chunk)
         if chunk >= EARLY:
@@ -218,11 +297,11 @@
     for hop in range(1, far + 1):
         for step in zip(*(chunks(d, hop) for d in (0, 1))):
             for direction, chunk in enumerate(step):
+                if hop == far or (direction == 0 and (hop > 1 or chunk >= EARLY)):
+                    arrived(hop, chunk)
                 if hop == 1 and chunk < EARLY:
                     early_copy(direction, chunk).wait_recv()
-                    rounded(early.at[direction, bounds[chunk][0]:bounds[chunk][1], :], direction, hop, chunk)
-                else:
-                    arrived(direction, hop, chunk).wait_recv()
+                    decoded(direction, chunk)
                 if hop + 1 <= far and chunk in chunks(direction, hop + 1):
                     ring(direction, hop, chunk).start()
                 share(direction, hop, chunk).start()
@@ -252,10 +331,13 @@
     all_of(out, nz * rows, share_send, share_recv).wait_recv()
     all_of(out, nz * rows, share_send, share_recv).wait_send()
     all_of(out, (nz - 1) * rows - 2 * bounds[EARLY - 1][1], ring_send, ring_recv.at[0]).wait_send()
-    for chunk in range(EARLY):
-        for direction in (0, 1):
+    for direction in (0, 1):
+        for part in (0, 1):
+            first_copy(direction, part).wait_send()
+        for chunk in range(EARLY):
             early_copy(direction, chunk).wait_send()
-    all_of(maxima, nrows - 1, max_send, max_recv).wait_send()
+    pair_copy(c).wait_send()
+    all_of(maxima, nz - 1, max_send, max_recv).wait_send()
 
     @pl.when(is_root)
     def _():
@@ -315,17 +397,24 @@
             pltpu.VMEM((1, small), jnp.float32),
             pltpu.VMEM((rows, cols), jnp.float32),
             pltpu.VMEM((rows, cols), jnp.float32),
-            pltpu.VMEM((2, early_rows, cols), jnp.float32),
+            pltpu.VMEM((3, early_rows, cols), jnp.bfloat16),
             pltpu.VMEM((rows, LANES), jnp.float32),
             pltpu.VMEM((8, cols), jnp.float32),
-            pltpu.VMEM((nrows, 1, cols), jnp.float32),
+            pltpu.VMEM((3, 2, 1, cols), jnp.float32),
+            pltpu.VMEM((2, 1, cols), jnp.float32),
+            pltpu.VMEM((nrows // 2, 1, cols), jnp.float32),
             pltpu.VMEM((8, LANES), jnp.float32),
             pltpu.VMEM((nrows, 8, LANES), jnp.float32),
             pltpu.VMEM((nwidth, 4 * nrows, LANES), jnp.float32),
             pltpu.VMEM((lines, LANES), jnp.float32),
+            pltpu.SemaphoreType.REGULAR((2, far - 1)),
             dma((3,)),
             dma((rows // LOAD,)),
             dma(()),
+            dma((2, 2)),
+            dma(()),
+            dma(()),
+            dma(()),
             dma(()),
             dma(()),
             dma(()),
@@ -336,7 +425,7 @@
             dma(()),
             dma((2, EARLY)),
             dma(()),
-            dma((2 * (far - 1) * nchunk + nchunk,)),
+            dma((far * nchunk - EARLY,)),
             dma(()),
             dma(()),
         ],

time: 101 us -> 96.2 us (0.952)
  Pallas kernels: 99.9 us -> 95.4 us
    pallas_call x1, Pallas kernels: 94 us -> 89.5 us  [shards(): pl.pallas_call(functools.partial(gather_kernel, nrows, nwidth, (rows, qd,...]
where the time goes in v4:
time: 96.2 us; the launch traced here: 96.1 us
  Pallas kernels  95.4 us (99%)
    pallas_call x1, Pallas kernels, shards(): pl.pallas_call(functools.partial(gather_kernel, nrows, nwidth, (rows, qd,...  89.5 us
    pallas_call x1, Pallas kernels, shards(): pl.pallas_call(functools.partial(write_kernel, (qd, kd)), out_shape=(jax....  5.9 us

profile of v4, /device:TPU:1, one launch (start us, length us, event | category | flops | bytes accessed | tf_op | source)
XLA Modules:
  0.0 96.1 jit_solution(641074478640527421)
XLA Ops:
  0.6 89.5 %gather.1 = (bf16[7168,1152]{1,0:T(8,128)(2,1)S(1)}, f32[7,128]{1,0:T(8,128)S(1)}, f32[1,128]{1,0:T(1,128)S(1)}, f32[1,128]{1,0:T(1,128)S(1)}, bf16[56,128]{1,0:T(8,128)(2,1)S(1)}) custom-call(f32[448,896]{1,0:T(8,128)} %refs_0_.1, f32[448,896]{1,0:T(8,128)} %refs_1_.1, f32[448,128]{1,0:T(8,128)} %refs_2_.1, f32[448,128]{1,0:T(8,128)} %refs_3_.1, ...), custom_call_target="tpu_custom_call" | custom-call | tf_op jit(solution)/shard_map/gather/pallas_call | solution.py:383
  90.2 5.9 %write.1 = (bf16[7168,896]{1,0:T(8,128)(2,1)}, bf16[7168,128]{1,0:T(8,128)(2,1)}, bf16[7168,128]{1,0:T(8,128)(2,1)}, f32[7,128]{1,0:T(8,128)}, f32[1,128]{1,0:T(...) custom-call(bf16[7168,1152]{1,0:T(8,128)(2,1)S(1)} %get-tuple-element.19.full, ...), custom_call_target="tpu_custom_call" | custom-call | tf_op jit(solution)/shard_map/write/pallas_call | solution.py:438

commit v5 on v4

--- a/solution.py
+++ b/solution.py
@@ -26,8 +26,8 @@
     (one_q, other_q, one_k, other_k, one_v, other_v, mix_hbm, norm_t_hbm, norm_s_hbm,
      out, scale_q, scale_k, scale_v, norm_out,
      mix, norm_t, norm_s, a_buf, b_buf, early, mixb, acc, firsts, pair, maxima, seg, tiles, gains, joined,
-     tokens, lead_sem, in_sem, first_send, first_recv, pair_send, pair_recv, max_send, max_recv, tile_send, tile_recv, gain_send, gain_recv, norm_send, norm_recv,
-     early_send, early_recv, ring_send, ring_recv, share_send, share_recv) = refs
+     tokens, lead_sem, in_sem, sent, first_recv, pair_recv, max_recv, tile_recv, gain_recv, norm_recv, early_recv, ring_recv,
+     share_recv) = refs
     rows, qd, kd = dims
     cols = qd + 2 * kd
     nz = nrows // 2
@@ -77,13 +77,13 @@
     def loads(step):
         span = pl.ds(step * LOAD, LOAD)
         return [
-            pltpu.make_async_copy(src.at[span, :], dst.at[span, pl.ds(at, n)], in_sem.at[step])
+            pltpu.make_async_copy(src.at[span, :], dst.at[span, pl.ds(at, n)], in_sem.at[min(step, 1)])
             for src, dst, at, n in parts
         ]
 
-    def wait_load(step):
-        both = a_buf.at[pl.ds(0, 2 * LOAD), :]
-        pltpu.make_async_copy(both, both, in_sem.at[step]).wait()
+    def wait_loads(count):
+        both = out.at[pl.ds(0, 4 * count), :]
+        pltpu.make_async_copy(both, both, in_sem.at[0 if count == LOAD else 1]).wait()
 
     def spread(at):
         n = min(LANES, rows - at)
@@ -119,19 +119,19 @@
     def early_copy(direction, chunk):
         span = pl.ds(bounds[chunk][0], bounds[chunk][1] - bounds[chunk][0])
         return pltpu.make_async_remote_copy(
-            src_ref=early.at[2, span, :], dst_ref=early.at[direction, span, :], send_sem=early_send,
-            recv_sem=early_recv.at[direction, chunk], device_id=ahead[direction], device_id_type=MESH)
+            src_ref=early.at[2, span, :], dst_ref=early.at[direction, span, :], send_sem=sent,
+            recv_sem=early_recv.at[chunk], device_id=ahead[direction], device_id_type=MESH)
 
     def first_copy(direction, part):
         return pltpu.make_async_remote_copy(
-            src_ref=firsts.at[2, part], dst_ref=firsts.at[direction, part], send_sem=first_send,
-            recv_sem=first_recv.at[direction, part], device_id=ahead[direction], device_id_type=MESH)
+            src_ref=firsts.at[2, part], dst_ref=firsts.at[direction, part], send_sem=sent,
+            recv_sem=first_recv.at[part], device_id=ahead[direction], device_id_type=MESH)
 
     for copy in loads(0):
         copy.start()
     for copy in leads:
         copy.wait()
-    wait_load(0)
+    wait_loads(LOAD)
     for step in range(1, rows // LOAD):
         for copy in loads(step):
             copy.start()
@@ -161,13 +161,13 @@
 
     for at in range(LANES, rows, LANES):
         spread(at)
+    wait_loads(rows - LOAD)
     for step in range(1, rows // LOAD):
-        wait_load(step)
         mixed(step)
 
     def pair_copy(core):
         return pltpu.make_async_remote_copy(
-            src_ref=pair.at[core], dst_ref=pair.at[core], send_sem=pair_send, recv_sem=pair_recv,
+            src_ref=pair.at[core], dst_ref=pair.at[core], send_sem=sent, recv_sem=pair_recv,
             device_id=partner, device_id_type=MESH)
 
     firsts[2, 1] = jnp.max(acc[...], axis=0, keepdims=True)
@@ -184,7 +184,7 @@
 
     def max_copy(i):
         return pltpu.make_async_remote_copy(
-            src_ref=maxima.at[z], dst_ref=maxima.at[z], send_sem=max_send, recv_sem=max_recv,
+            src_ref=maxima.at[z], dst_ref=maxima.at[z], send_sem=sent, recv_sem=max_recv,
             device_id=row_peer(2 * i), device_id_type=MESH)
 
     def all_of(ref, count, send_sem, recv_sem):
@@ -212,24 +212,24 @@
 
     def tile_copy(source):
         return pltpu.make_async_remote_copy(
-            src_ref=tiles.at[source], dst_ref=tiles.at[source], send_sem=tile_send, recv_sem=tile_recv,
+            src_ref=tiles.at[source], dst_ref=tiles.at[source], send_sem=sent, recv_sem=tile_recv,
             device_id={"rows": root}, device_id_type=MESH)
 
     def gain_copy(i):
         return pltpu.make_async_remote_copy(
-            src_ref=gains.at[w], dst_ref=gains.at[w], send_sem=gain_send, recv_sem=gain_recv,
+            src_ref=gains.at[w], dst_ref=gains.at[w], send_sem=sent, recv_sem=gain_recv,
             device_id=width_peer(i), device_id_type=MESH)
 
     def norm_copy(i):
         return pltpu.make_async_remote_copy(
-            src_ref=norm_out, dst_ref=norm_out, send_sem=norm_send, recv_sem=norm_recv,
+            src_ref=norm_out, dst_ref=norm_out, send_sem=sent, recv_sem=norm_recv,
             device_id=row_peer(i), device_id_type=MESH)
 
     @pl.when(jnp.logical_not(is_root))
     def _():
         tile_copy(r).start()
 
-    all_of(maxima, nz - 1, max_send, max_recv).wait_recv()
+    all_of(maxima, nz - 1, sent, max_recv).wait_recv()
     scale = maxima[0]
     for i in range(1, nz):
         scale = jnp.maximum(scale, maxima[i])
@@ -245,18 +245,18 @@
     def ring(direction, hop, chunk):
         ref = out.at[place(direction, hop, chunk), :]
         return pltpu.make_async_remote_copy(
-            src_ref=ref, dst_ref=ref, send_sem=ring_send, recv_sem=ring_recv.at[landing(hop, chunk)],
+            src_ref=ref, dst_ref=ref, send_sem=sent, recv_sem=ring_recv.at[landing(hop, chunk)],
             device_id=ahead[direction], device_id_type=MESH)
 
     def arrived(hop, chunk):
         lo, hi = bounds[chunk]
         sides = 2 if hop < far else 1
-        all_of(out, sides * (hi - lo), ring_send, ring_recv.at[landing(hop - 1, chunk)]).wait_recv()
+        all_of(out, sides * (hi - lo), sent, ring_recv.at[landing(hop - 1, chunk)]).wait_recv()
 
     def share(direction, hop, chunk):
         ref = out.at[place(direction, hop, chunk), :]
         return pltpu.make_async_remote_copy(
-            src_ref=ref, dst_ref=ref, send_sem=share_send, recv_sem=share_recv,
+            src_ref=ref, dst_ref=ref, send_sem=sent, recv_sem=share_recv,
             device_id=partner, device_id_type=MESH)
 
     def chunks(direction, hop):
@@ -272,8 +272,6 @@
 
     def decoded(direction, chunk):
         part = min(chunk, 1)
-        if chunk < 2:
-            first_copy(direction, part).wait_recv()
         factor = jnp.maximum(firsts[direction, part], TINY) / scale
         at_rows = place(direction, 1, chunk)
         for at in range(0, cols, LANES):
@@ -294,22 +292,32 @@
     scale_k[...] = scale[:, qd:qd + kd]
     scale_v[...] = scale[:, qd + kd:]
 
+    moved = nchunk // 2 - 1
+
     for hop in range(1, far + 1):
         for step in zip(*(chunks(d, hop) for d in (0, 1))):
             for direction, chunk in enumerate(step):
                 if hop == far or (direction == 0 and (hop > 1 or chunk >= EARLY)):
                     arrived(hop, chunk)
                 if hop == 1 and chunk < EARLY:
-                    early_copy(direction, chunk).wait_recv()
+                    if direction == 0:
+                        lo, hi = bounds[chunk]
+                        if chunk < 2:
+                            all_of(pair, 2, sent, first_recv.at[chunk]).wait_recv()
+                        all_of(out, 2 * (hi - lo), sent, early_recv.at[chunk]).wait_recv()
                     decoded(direction, chunk)
-                if hop + 1 <= far and chunk in chunks(direction, hop + 1):
+                if hop + 1 == far and chunk == moved:
+                    @pl.when((z != nz - 1) if direction == 0 else (z == 1))
+                    def _():
+                        ring(direction, hop, chunk).start()
+                elif hop + 1 <= far and chunk in chunks(direction, hop + 1):
                     ring(direction, hop, chunk).start()
                 share(direction, hop, chunk).start()
 
         if hop == 1:
             @pl.when(is_root)
             def _():
-                all_of(tiles, nrows - 1, tile_send, tile_recv).wait_recv()
+                all_of(tiles, nrows - 1, sent, tile_recv).wait_recv()
                 for g in range(nrows // 2):
                     gains[w, 8 * g:8 * g + 8, :] = tiles[2 * g] + tiles[2 * g + 1]
                 for i in range(1, nwidth):
@@ -317,7 +325,7 @@
         if hop == 2:
             @pl.when(is_root)
             def _():
-                all_of(gains, nwidth - 1, gain_send, gain_recv).wait_recv()
+                all_of(gains, nwidth - 1, sent, gain_recv).wait_recv()
                 per = 2 * nwidth * small // LANES
                 for g in range(nrows // 2):
                     full = gains[0, 8 * g:8 * g + 8, :]
@@ -328,20 +336,25 @@
                 for i in range(1, nrows):
                     norm_copy(i).start()
 
-    all_of(out, nz * rows, share_send, share_recv).wait_recv()
-    all_of(out, nz * rows, share_send, share_recv).wait_send()
-    all_of(out, (nz - 1) * rows - 2 * bounds[EARLY - 1][1], ring_send, ring_recv.at[0]).wait_send()
+    all_of(out, nz * rows, sent, share_recv).wait_recv()
+    all_of(out, nz * rows, sent, share_recv).wait_send()
+    length = bounds[moved][1] - bounds[moved][0]
+    all_of(out, (nz - 1) * rows - 2 * bounds[EARLY - 1][1] - length, sent, ring_recv.at[0]).wait_send()
+    for sender in (z != nz - 1, z == 1):
+        @pl.when(sender)
+        def _():
+            all_of(out, length, sent, ring_recv.at[0]).wait_send()
     for direction in (0, 1):
         for part in (0, 1):
             first_copy(direction, part).wait_send()
         for chunk in range(EARLY):
             early_copy(direction, chunk).wait_send()
     pair_copy(c).wait_send()
-    all_of(maxima, nz - 1, max_send, max_recv).wait_send()
+    all_of(maxima, nz - 1, sent, max_recv).wait_send()
 
     @pl.when(is_root)
     def _():
-        all_of(gains, nwidth - 1, gain_send, gain_recv).wait_send()
+        all_of(gains, nwidth - 1, sent, gain_recv).wait_send()
         for i in range(1, nrows):
             norm_copy(i).wait_send()
 
@@ -409,24 +422,16 @@
             pltpu.VMEM((lines, LANES), jnp.float32),
             pltpu.SemaphoreType.REGULAR((2, far - 1)),
             dma((3,)),
-            dma((rows // LOAD,)),
-            dma(()),
-            dma((2, 2)),
-            dma(()),
-            dma(()),
-            dma(()),
-            dma(()),
-            dma(()),
-            dma(()),
-            dma(()),
-            dma(()),
-            dma(()),
-            dma(()),
-            dma(()),
-            dma((2, EARLY)),
-            dma(()),
+            dma((2,)),
+            dma(()),
+            dma((2,)),
+            dma(()),
+            dma(()),
+            dma(()),
+            dma(()),
+            dma(()),
+            dma((EARLY,)),
             dma((far * nchunk - EARLY,)),
-            dma(()),
             dma(()),
         ],
         compiler_params=pltpu.CompilerParams(

time: 96.2 us -> 95.5 us (level)
  no operation moved by 1% of the time
where the time goes in v5:
time: 95.5 us; the launch traced here: 95.4 us
  Pallas kernels  94.7 us (99%)
    pallas_call x1, Pallas kernels, shards(): pl.pallas_call(functools.partial(gather_kernel, nrows, nwidth, (rows, qd,...  88.8 us
    pallas_call x1, Pallas kernels, shards(): pl.pallas_call(functools.partial(write_kernel, (qd, kd)), out_shape=(jax....  5.9 us

profile of v5, /device:TPU:1, one launch (start us, length us, event | category | flops | bytes accessed | tf_op | source)
XLA Modules:
  0.0 95.4 jit_solution(10286548200844149405)
XLA Ops:
  0.6 88.8 %gather.1 = (bf16[7168,1152]{1,0:T(8,128)(2,1)S(1)}, f32[7,128]{1,0:T(8,128)S(1)}, f32[1,128]{1,0:T(1,128)S(1)}, f32[1,128]{1,0:T(1,128)S(1)}, bf16[56,128]{1,0:T(8,128)(2,1)S(1)}) custom-call(f32[448,896]{1,0:T(8,128)} %refs_0_.1, f32[448,896]{1,0:T(8,128)} %refs_1_.1, f32[448,128]{1,0:T(8,128)} %refs_2_.1, f32[448,128]{1,0:T(8,128)} %refs_3_.1, ...), custom_call_target="tpu_custom_call" | custom-call | tf_op jit(solution)/shard_map/gather/pallas_call | solution.py:396
  89.5 5.9 %write.1 = (bf16[7168,896]{1,0:T(8,128)(2,1)}, bf16[7168,128]{1,0:T(8,128)(2,1)}, bf16[7168,128]{1,0:T(8,128)(2,1)}, f32[7,128]{1,0:T(8,128)}, f32[1,128]{1,0:T(...) custom-call(bf16[7168,1152]{1,0:T(8,128)(2,1)S(1)} %get-tuple-element.19.full, ...), custom_call_target="tpu_custom_call" | custom-call | tf_op jit(solution)/shard_map/write/pallas_call | solution.py:443

commit v6 on v5

--- a/solution.py
+++ b/solution.py
@@ -270,20 +270,23 @@
             lanes = slice(at, at + LANES)
             out[at_rows, lanes] = (source[:, lanes] / scale[:, lanes]).astype(out.dtype)
 
-    def decoded(direction, chunk):
+    def decoded(direction, hop, chunk):
+        slot = direction if hop else 2
         part = min(chunk, 1)
-        factor = jnp.maximum(firsts[direction, part], TINY) / scale
-        at_rows = place(direction, 1, chunk)
+        factor = jnp.maximum(firsts[slot, part], TINY) / scale
+        at_rows = place(direction, hop, chunk)
         for at in range(0, cols, LANES):
             lanes = slice(at, at + LANES)
-            code = early[direction, bounds[chunk][0]:bounds[chunk][1], lanes].astype(jnp.float32)
+            code = early[slot, bounds[chunk][0]:bounds[chunk][1], lanes].astype(jnp.float32)
             size = jnp.exp2(jnp.log2(jnp.abs(code)) * (1.0 / 16.0) - 126.0 / 16.0)
             out[at_rows, lanes] = (jnp.where(code < 0.0, -size, size) * factor[:, lanes]).astype(out.dtype)
 
     for chunk in (*range(EARLY, nchunk), *range(EARLY)):
-        lo, hi = bounds[chunk]
-        rounded(a_buf.at[lo:hi, :], 0, 0, chunk)
-        if chunk >= EARLY:
+        if chunk < EARLY:
+            decoded(0, 0, chunk)
+        else:
+            lo, hi = bounds[chunk]
+            rounded(a_buf.at[lo:hi, :], 0, 0, chunk)
             for direction in (0, 1):
                 ring(direction, 0, chunk).start()
         share(0, 0, chunk).start()
@@ -305,7 +308,7 @@
                         if chunk < 2:
                             all_of(pair, 2, sent, first_recv.at[chunk]).wait_recv()
                         all_of(out, 2 * (hi - lo), sent, early_recv.at[chunk]).wait_recv()
-                    decoded(direction, chunk)
+                    decoded(direction, hop, chunk)
                 if hop + 1 == far and chunk == moved:
                     @pl.when((z != nz - 1) if direction == 0 else (z == 1))
                     def _():

time: 95.5 us -> 95.5 us (level)
  no operation moved by 1% of the time
where the time goes in v6:
time: 95.5 us; the launch traced here: 95.4 us
  Pallas kernels  94.7 us (99%)
    pallas_call x1, Pallas kernels, shards(): pl.pallas_call(functools.partial(gather_kernel, nrows, nwidth, (rows, qd,...  88.8 us
    pallas_call x1, Pallas kernels, shards(): pl.pallas_call(functools.partial(write_kernel, (qd, kd)), out_shape=(jax....  5.9 us

profile of v6, /device:TPU:1, one launch (start us, length us, event | category | flops | bytes accessed | tf_op | source)
XLA Modules:
  0.0 95.4 jit_solution(5929460728655590929)
XLA Ops:
  0.6 88.8 %gather.1 = (bf16[7168,1152]{1,0:T(8,128)(2,1)S(1)}, f32[7,128]{1,0:T(8,128)S(1)}, f32[1,128]{1,0:T(1,128)S(1)}, f32[1,128]{1,0:T(1,128)S(1)}, bf16[56,128]{1,0:T(8,128)(2,1)S(1)}) custom-call(f32[448,896]{1,0:T(8,128)} %refs_0_.1, f32[448,896]{1,0:T(8,128)} %refs_1_.1, f32[448,128]{1,0:T(8,128)} %refs_2_.1, f32[448,128]{1,0:T(8,128)} %refs_3_.1, ...), custom_call_target="tpu_custom_call" | custom-call | tf_op jit(solution)/shard_map/gather/pallas_call | solution.py:399
  89.5 5.9 %write.1 = (bf16[7168,896]{1,0:T(8,128)(2,1)}, bf16[7168,128]{1,0:T(8,128)(2,1)}, bf16[7168,128]{1,0:T(8,128)(2,1)}, f32[7,128]{1,0:T(8,128)}, f32[1,128]{1,0:T(...) custom-call(bf16[7168,1152]{1,0:T(8,128)(2,1)S(1)} %get-tuple-element.19.full, ...), custom_call_target="tpu_custom_call" | custom-call | tf_op jit(solution)/shard_map/write/pallas_call | solution.py:446
